TPU v7x, 256 devices: a whole 4x4x8 slice. The times are simulated.
256 devices in a mesh: probe: 4 (over y), space: 64 (over x, z, core).
Axes of the slice: x: 4, y: 4, z: 8, core: 2. Of those that a mesh axis runs over, the one named last changes fastest.
Arguments:
- probe_signs: int32 [192, 512, 1024], P('probe', 'space'), may hold values from 0 to 1, as said below
- sensor_mask: int32 [512, 1024], P('space'), may hold values 0 or 1
- sensor_weight: float32 [512, 1024], P('space'), may hold values from 1 to 30
- prior_mass: float32 [512, 1024], P('space'), may hold values from 0.02 to 0.5
Outputs:
- solution: float32 [192, 512, 1024], P('probe', 'space')
- trace_cell: float32 [], replicated
Inputs may be any that keep to these rules, and one draw needn't show every extreme that they name: `probe_signs`: each entry is 0 or 1; the probe's sign is twice the entry minus one.
All inputs are finite; a program needn't handle non-finite values. No bound on the sum of `sensor_mask` on one device may be relied on, other than what follows from the above.
Results may differ from a plain program's by a relative error of at most 0.0001.
Values sent between devices are 32-bit elements; how exact they have to be, the bound alone decides.
No kernel may reach another device: no remote copies, remote signals or barrier semaphores. Data moves between devices by JAX's collectives and lax.ppermute only.
A program may use at most 64 MiB of HBM per device.

v0:
```python
import jax
import jax.numpy as jnp
from jax import lax
from jax.sharding import PartitionSpec as P

ITERS = 4


def with_halo(cells, sides, width):
    for axis, dim in sides:
        count = lax.axis_size(axis)
        ends = count - 1
        head = lax.slice_in_dim(cells, 0, width, axis=dim)
        tail = lax.slice_in_dim(cells, cells.shape[dim] - width, cells.shape[dim], axis=dim)
        cells = jnp.concatenate(
            [
                lax.ppermute(tail, axis, [(i, (i + 1) % count) for i in range(ends)]),
                cells,
                lax.ppermute(head, axis, [((i + 1) % count, i) for i in range(ends)]),
            ],
            axis=dim,
        )
    return cells


def sent_to_all(array, axis):
    copies = jnp.broadcast_to(array, (lax.axis_size(axis), *array.shape))
    return lax.all_to_all(copies, axis, split_axis=0, concat_axis=0, tiled=True)


def of_everyone(array, axis):
    everything = sent_to_all(array, axis)
    return jnp.sum(everything, axis=0)


def together(arrays, axis):
    ends = [0]
    for a in arrays:
        ends.append(ends[-1] + a.size)
    subtotal = of_everyone(jnp.concatenate([a.ravel() for a in arrays]), axis)
    return tuple((subtotal[b:e].reshape(a.shape) for a, b, e in zip(arrays, ends, ends[1:])))


def operate(vector_in, diagonal):
    padded = with_halo(vector_in, (("space", 1),), 1)
    padded = jnp.pad(padded, ((0, 0), (0, 0), (1, 1)))
    beside = padded[:, 2:, 1:-1] + padded[:, :-2, 1:-1]
    beside = beside + padded[:, 1:-1, 2:] + padded[:, 1:-1, :-2]
    return (4.0 + diagonal) * vector_in - beside


def per_probe(values):
    return jnp.sum(values, axis=(1, 2))


def two_sums(residual, applied):
    return together((per_probe(residual * residual), per_probe(residual * applied)), "space")


def on_device(probe_signs, sensor_mask, sensor_weight, prior_mass):
    probes = 2.0 * probe_signs.astype(jnp.float32) - 1.0
    diagonal = sensor_mask.astype(jnp.float32) * sensor_weight + prior_mass
    solution = jnp.zeros_like(probes)
    residual = probes
    applied = operate(residual, diagonal)
    norm_now, curvature = two_sums(residual, applied)
    step_len = norm_now / curvature
    direction = residual
    applied_dir = applied
    for iterate in range(ITERS):
        solution = solution + step_len[:, None, None] * direction
        residual = residual - step_len[:, None, None] * applied_dir
        if iterate + 1 < ITERS:
            applied = operate(residual, diagonal)
            norm_next, curvature = two_sums(residual, applied)
            step_ratio = norm_next / norm_now
            step_len = norm_next / (curvature - step_ratio * norm_next / step_len)
            direction = residual + step_ratio[:, None, None] * direction
            applied_dir = applied + step_ratio[:, None, None] * applied_dir
            norm_now = norm_next
    local_part = jnp.sum(probes * solution)
    strip_sum = of_everyone(local_part, "space")
    trace_sum = of_everyone(strip_sum, "probe")
    cells = (
        probes.shape[0]
        * lax.axis_size("probe")
        * probes.shape[1]
        * lax.axis_size("space")
        * probes.shape[2]
    )
    return (solution, trace_sum / float(cells))


def solution(mesh):
    return jax.shard_map(
        on_device,
        mesh=mesh,
        in_specs=(P("probe", "space", None), P("space", None), P("space", None), P("space", None)),
        out_specs=(P("probe", "space", None), P()),
        check_vma=False,
    )
```

profile of v0, /device:TPU:1, one launch (start us, length us, event | category | flops | bytes accessed | tf_op | source)
XLA Modules:
  0.0 171.2 jit_solution(14906350884955168154)
XLA Ops:
  0.6 0.0 copy-start.6
  0.6 0.0 copy-start.7
  0.7 0.0 copy-start.8
  0.7 2.5 %fusion.12 = f32[48,8,1024]{2,0,1:T(8,128)S(1)} fusion(s32[48,8,1024]{2,1,0:T(8,128)} %param.4), kind=kLoop, calls=%fused_computation.39 | loop fusion | flops 1179648 | bytes 3145728 | tf_op jit(solution)/shard_map/sub | solution.py:61
  3.2 4.9 %collective-permute-start.1 = (f32[48,1,1024]{2,0,1:T(8,128)S(1)}, f32[48,1,1024]{2,0,1:T(8,128)S(1)}, u32[]{:S(2)}, u32[]{:S(2)}) collective-permute-start(f32[48,1,1024]{2,0,1:T(8,128)S(1)} %get-tuple-element.34), channel_id=1, source_target_pairs={{0,1},{1,2},{2,3},{3,4},{4,5},{5,6},{6,7},{7,8},{8,9},{9,10},{10,1... | collective-permute-start | bytes 589832 | tf_op jit(solution)/shard_map/ppermute | solution.py:17
  8.2 1.9 %collective-permute-start = (f32[48,1,1024]{2,0,1:T(8,128)S(1)}, f32[48,1,1024]{2,0,1:T(8,128)S(1)}, u32[]{:S(2)}, u32[]{:S(2)}) collective-permute-start(f32[48,1,1024]{2,0,1:T(8,128)S(1)} %get-tuple-element.35), channel_id=1, source_target_pairs={{1,0},{2,1},{3,2},{4,3},{5,4},{6,5},{7,6},{8,7},{9,8},{10,9},{11,1... | collective-permute-start | bytes 589832 | tf_op jit(solution)/shard_map/ppermute | solution.py:19
  10.1 0.0 copy-done.6
  10.1 0.0 copy-done.7
  10.1 0.0 copy-done.8
  10.1 0.0 copy-start.3
  10.1 0.0 copy-start.2
  10.2 0.6 collective-permute-done.1
  10.7 4.4 %collective-permute-done = f32[48,1,1024]{2,0,1:T(8,128)S(1)} collective-permute-done((f32[48,1,1024]{2,0,1:T(8,128)S(1)}, f32[48,1,1024]{2,0,1:T(8,128)S(1)}, u32[]{:S(2)}, u32[]{:S(2)}) %collective-permute-start) | collective-permute-done | bytes 196640 | tf_op jit(solution)/shard_map/ppermute | solution.py:19
  15.1 0.6 select_maximum_fusion.6
  15.8 2.8 %multiply_reduce_fusion.7 = (f32[48]{0:T(128)S(1)}, f32[48]{0:T(128)S(1)}, f32[48,8,1024]{2,0,1:T(8,128)}) fusion(s32[48,8,1024]{2,1,0:T(8,128)S(1)} %copy-done.2, f32[48,10,1026]{2,0,1:T(8,128)S(1)} %select_maximum_fusion.6, f32[48,8,1024]{2,0,1:T(8,128)S(1)} %fusion.12, f32[48,1,1024]{2,0,1:T(8,128)S(1)} %collective-permute-done.1, ...), kind=kLoop, calls=%fused_computation.52 | loop fusion | flops 5504928 | bytes 8290688 | tf_op jit(solution)/shard_map/reduce_sum | solution.py:53
  18.6 0.1 pad_maximum_fusion.8
  18.7 20.6 %all_to_all.36 = f32[64,1,96]{2,1,0:T(1,128)S(1)} all-to-all(f32[64,1,96]{2,1,0:T(1,128)S(1)} %broadcast_in_dim.12), channel_id=1, replica_groups=mesh['probe'=4,'space'=64] {'space'}, dimensions={0} | all-to-all | bytes 49152 | tf_op jit(solution)/shard_map/all_to_all | solution.py:28
  39.3 0.1 slice_divide_fusion.1
  39.3 2.6 %multiply_subtract_fusion.2 = f32[48,8,1024]{2,0,1:T(8,128)S(1)} fusion(f32[48,8,1024]{2,0,1:T(8,128)} %get-tuple-element.27, f32[48]{0:T(128)S(1)} %slice_divide_fusion.1, s32[48,8,1024]{2,1,0:T(8,128)S(1)} %copy-done.2), kind=kLoop, calls=%fused_computation.50 | loop fusion | flops 1966080 | bytes 4718784 | tf_op jit(solution)/shard_map/sub | solution.py:72
  42.0 2.8 %collective-permute-start.3 = (f32[48,1,1024]{2,0,1:T(8,128)S(1)}, f32[48,1,1024]{2,0,1:T(8,128)S(1)}, u32[]{:S(2)}, u32[]{:S(2)}) collective-permute-start(f32[48,1,1024]{2,0,1:T(8,128)S(1)} %get-tuple-element.32), channel_id=1, source_target_pairs={{0,1},{1,2},{2,3},{3,4},{4,5},{5,6},{6,7},{7,8},{8,9},{9,10},{10,1... | collective-permute-start | bytes 589832 | tf_op jit(solution)/shard_map/ppermute | solution.py:17
  44.8 1.9 %collective-permute-start.2 = (f32[48,1,1024]{2,0,1:T(8,128)S(1)}, f32[48,1,1024]{2,0,1:T(8,128)S(1)}, u32[]{:S(2)}, u32[]{:S(2)}) collective-permute-start(f32[48,1,1024]{2,0,1:T(8,128)S(1)} %get-tuple-element.33), channel_id=1, source_target_pairs={{1,0},{2,1},{3,2},{4,3},{5,4},{6,5},{7,6},{8,7},{9,8},{10,9},{11,1... | collective-permute-start | bytes 589832 | tf_op jit(solution)/shard_map/ppermute | solution.py:19
  46.8 0.7 collective-permute-done.3
  47.4 4.4 %collective-permute-done.2 = f32[48,1,1024]{2,0,1:T(8,128)S(1)} collective-permute-done((f32[48,1,1024]{2,0,1:T(8,128)S(1)}, f32[48,1,1024]{2,0,1:T(8,128)S(1)}, u32[]{:S(2)}, u32[]{:S(2)}) %collective-permute-start.2) | collective-permute-done | bytes 196640 | tf_op jit(solution)/shard_map/ppermute | solution.py:19
  51.8 0.6 select_maximum_fusion.4
  52.5 2.0 %multiply_reduce_fusion.5 = (f32[48]{0:T(128)S(1)}, f32[48]{0:T(128)S(1)}, f32[48,8,1024]{2,0,1:T(8,128)}) fusion(f32[48,8,1024]{2,0,1:T(8,128)S(1)} %multiply_subtract_fusion.2, f32[48,10,1026]{2,0,1:T(8,128)S(1)} %select_maximum_fusion.4, f32[48,1,1024]{2,0,1:T(8,128)S(1)} %collective-permute-done.3, f32[48,1,1024]{2,0,1:T(8,128)S(1)} %collective-permute-done.2, ...), kind=kLoop, calls=%fused_computation.49 | loop fusion | flops 4325280 | bytes 6717824 | tf_op jit(solution)/shard_map/reduce_sum | solution.py:53
  54.5 0.1 pad_maximum_fusion.9
  54.6 17.2 %all_to_all.37 = f32[64,1,96]{2,1,0:T(1,128)S(1)} all-to-all(f32[64,1,96]{2,1,0:T(1,128)S(1)} %broadcast_in_dim.13), channel_id=1, replica_groups=mesh['probe'=4,'space'=64] {'space'}, dimensions={0} | all-to-all | bytes 49152 | tf_op jit(solution)/shard_map/all_to_all | solution.py:28
  71.8 0.6 slice_divide_fusion.5
  72.4 2.4 %multiply_subtract_fusion.1 = f32[48,8,1024]{2,0,1:T(8,128)S(1)} fusion(f32[48,8,1024]{2,0,1:T(8,128)S(1)} %multiply_subtract_fusion.2, f32[48]{0:T(128)S(1)} %get-tuple-element.23, f32[48,8,1024]{2,0,1:T(8,128)} %get-tuple-element.26, f32[48,8,1024]{2,0,1:T(8,128)} %get-tuple-element.27, f32[48]{0:T(128)S(1)} %get-tuple-element.25), kind=kLoop, calls=%fused_computation.46 | loop fusion | flops 1572864 | bytes 6291840 | tf_op jit(solution)/shard_map/sub | solution.py:72
  74.9 2.8 %collective-permute-start.5 = (f32[48,1,1024]{2,0,1:T(8,128)S(1)}, f32[48,1,1024]{2,0,1:T(8,128)S(1)}, u32[]{:S(2)}, u32[]{:S(2)}) collective-permute-start(f32[48,1,1024]{2,0,1:T(8,128)S(1)} %get-tuple-element.30), channel_id=1, source_target_pairs={{0,1},{1,2},{2,3},{3,4},{4,5},{5,6},{6,7},{7,8},{8,9},{9,10},{10,1... | collective-permute-start | bytes 589832 | tf_op jit(solution)/shard_map/ppermute | solution.py:17
  77.7 1.9 %collective-permute-start.4 = (f32[48,1,1024]{2,0,1:T(8,128)S(1)}, f32[48,1,1024]{2,0,1:T(8,128)S(1)}, u32[]{:S(2)}, u32[]{:S(2)}) collective-permute-start(f32[48,1,1024]{2,0,1:T(8,128)S(1)} %get-tuple-element.31), channel_id=1, source_target_pairs={{1,0},{2,1},{3,2},{4,3},{5,4},{6,5},{7,6},{8,7},{9,8},{10,9},{11,1... | collective-permute-start | bytes 589832 | tf_op jit(solution)/shard_map/ppermute | solution.py:19
  79.6 0.7 collective-permute-done.5
  80.3 4.4 %collective-permute-done.4 = f32[48,1,1024]{2,0,1:T(8,128)S(1)} collective-permute-done((f32[48,1,1024]{2,0,1:T(8,128)S(1)}, f32[48,1,1024]{2,0,1:T(8,128)S(1)}, u32[]{:S(2)}, u32[]{:S(2)}) %collective-permute-start.4) | collective-permute-done | bytes 196640 | tf_op jit(solution)/shard_map/ppermute | solution.py:19
  84.7 0.6 select_maximum_fusion.2
  85.3 0.8 multiply_reduce_fusion.3
  86.2 0.5 copy-done
  86.7 0.1 pad_maximum_fusion.10
  86.8 17.1 %all_to_all.38 = f32[64,1,96]{2,1,0:T(1,128)} all-to-all(f32[64,1,96]{2,1,0:T(1,128)S(1)} %broadcast_in_dim.14), channel_id=1, replica_groups=mesh['probe'=4,'space'=64] {'space'}, dimensions={0} | all-to-all | bytes 49152 | tf_op jit(solution)/shard_map/all_to_all | solution.py:28
  104.0 0.8 reduce_sum.143
  104.7 1.2 slice_divide_fusion.3
  106.0 3.9 %multiply_subtract_fusion = f32[48,8,1024]{2,0,1:T(8,128)S(1)} fusion(f32[48,8,1024]{2,0,1:T(8,128)S(1)} %multiply_subtract_fusion.1, f32[48]{0:T(128)S(1)} %get-tuple-element.22, f32[48]{0:T(128)S(1)} %get-tuple-element.20, f32[48,8,1024]{2,0,1:T(8,128)} %get-tuple-element.26, f32[48,8,1024]{2,0,1:T(8,128)} %get-tuple-element.27, ...), kind=kLoop, calls=%fused_computation.43 | loop fusion | flops 5111808 | bytes 9863744 | tf_op jit(solution)/shard_map/sub | solution.py:72
  109.9 0.0 copy-start.1
  110.0 3.0 %collective-permute-start.7 = (f32[48,1,1024]{2,0,1:T(8,128)S(1)}, f32[48,1,1024]{2,0,1:T(8,128)S(1)}, u32[]{:S(2)}, u32[]{:S(2)}) collective-permute-start(f32[48,1,1024]{2,0,1:T(8,128)S(1)} %get-tuple-element.28), channel_id=1, source_target_pairs={{0,1},{1,2},{2,3},{3,4},{4,5},{5,6},{6,7},{7,8},{8,9},{9,10},{10,1... | collective-permute-start | bytes 589832 | tf_op jit(solution)/shard_map/ppermute | solution.py:17
  113.0 1.9 %collective-permute-start.6 = (f32[48,1,1024]{2,0,1:T(8,128)S(1)}, f32[48,1,1024]{2,0,1:T(8,128)S(1)}, u32[]{:S(2)}, u32[]{:S(2)}) collective-permute-start(f32[48,1,1024]{2,0,1:T(8,128)S(1)} %get-tuple-element.29), channel_id=1, source_target_pairs={{1,0},{2,1},{3,2},{4,3},{5,4},{6,5},{7,6},{8,7},{9,8},{10,9},{11,1... | collective-permute-start | bytes 589832 | tf_op jit(solution)/shard_map/ppermute | solution.py:19
  114.9 0.7 collective-permute-done.7
  115.6 4.4 %collective-permute-done.6 = f32[48,1,1024]{2,0,1:T(8,128)S(1)} collective-permute-done((f32[48,1,1024]{2,0,1:T(8,128)S(1)}, f32[48,1,1024]{2,0,1:T(8,128)S(1)}, u32[]{:S(2)}, u32[]{:S(2)}) %collective-permute-start.6) | collective-permute-done | bytes 196640 | tf_op jit(solution)/shard_map/ppermute | solution.py:19
  120.0 0.6 select_maximum_fusion
  120.6 0.0 copy-done.1
  120.6 0.0 copy-done.5
  120.6 0.0 copy-start.15
  120.7 0.8 multiply_reduce_fusion.1
  121.5 0.1 pad_maximum_fusion.11
  121.6 17.2 %all_to_all.39 = f32[64,1,96]{2,1,0:T(1,128)S(1)} all-to-all(f32[64,1,96]{2,1,0:T(1,128)S(1)} %broadcast_in_dim.15), channel_id=1, replica_groups=mesh['probe'=4,'space'=64] {'space'}, dimensions={0} | all-to-all | bytes 49152 | tf_op jit(solution)/shard_map/all_to_all | solution.py:28
  138.8 0.0 copy-done.15
  138.8 0.1 subtract_divide_fusion
  138.9 5.1 %multiply_reduce_fusion = (f32[]{:T(128)}, f32[48,8,1024]{2,0,1:T(8,128)}) fusion(s32[48,8,1024]{2,1,0:T(8,128)} %param.4, f32[48,8,1024]{2,0,1:T(8,128)} %copy-done.1, f32[48]{0:T(128)S(1)} %get-tuple-element.19, f32[48]{0:T(128)S(1)} %get-tuple-element.18, f32[48,8,1024]{2,0,1:T(8,128)S(1)} %multiply_subtract_fusion.1, f32[48]{0:T(128)S(1)} %copy-done.12, ...), kind=kLoop, calls=%fused_computation.40 | loop fusion | flops 7077887 | bytes 7865668 | tf_op jit(solution)/shard_map/reduce_sum | solution.py:81
  144.0 1.3 broadcast_in_dim.16
  145.2 4.7 %all-to-all-start.4 = ((f32[64,1,1]{2,1,0:T(1,128)}), f32[64,1,1]{2,1,0:T(1,128)S(1)}, u32[]{:S(2)}, u32[]{:S(2)}) async-start(f32[64,1,1]{2,1,0:T(1,128)} %broadcast_in_dim.16), calls=%async_computation.4 | async-start | bytes 65536 | tf_op jit(solution)/shard_map/all_to_all | solution.py:28
  149.9 3.5 %copy.17 = f32[48,8,1024]{2,1,0:T(8,128)} copy(f32[48,8,1024]{2,0,1:T(8,128)} %get-tuple-element.17) | data formatting | bytes 3145728
  153.4 6.0 %all-to-all-done.4 = f32[64,1,1]{2,1,0:T(1,128)S(1)} async-done(((f32[64,1,1]{2,1,0:T(1,128)}), f32[64,1,1]{2,1,0:T(1,128)S(1)}, u32[]{:S(2)}, u32[]{:S(2)}) %all-to-all-start.4) | async-done | bytes 288 | tf_op jit(solution)/shard_map/all_to_all | solution.py:28
  159.3 0.7 reduce_sum.148
  160.0 0.6 broadcast_in_dim.17
  160.7 8.1 %all_to_all.40 = f32[4,1,1]{2,1,0:T(1,128)S(1)} all-to-all(f32[4,1,1]{2,1,0:T(1,128)S(1)} %broadcast_in_dim.17), channel_id=1, replica_groups=mesh['probe'=4,'space'=64] {'probe'}, dimensions={0} | all-to-all | bytes 32 | tf_op jit(solution)/shard_map/all_to_all | solution.py:28
  168.8 0.6 reduce_sum.149
  (30 shorter events, 0.3 us)
Async XLA Ops:
  0.6 9.5 %copy-start.6 = (f32[8,1024]{1,0:T(8,128)S(1)}, f32[8,1024]{1,0:T(8,128)}, u32[]{:S(2)}) copy-start(f32[8,1024]{1,0:T(8,128)} %param.7) | copy-start | bytes 98308
  0.6 9.5 %copy-start.7 = (f32[8,1024]{1,0:T(8,128)S(1)}, f32[8,1024]{1,0:T(8,128)}, u32[]{:S(2)}) copy-start(f32[8,1024]{1,0:T(8,128)} %param.6) | copy-start | bytes 98308
  0.7 9.5 %copy-start.8 = (s32[8,1024]{1,0:T(8,128)S(1)}, s32[8,1024]{1,0:T(8,128)}, u32[]{:S(2)}) copy-start(s32[8,1024]{1,0:T(8,128)} %param.5) | copy-start | bytes 98308
  3.2 7.5 %collective-permute-start.1 = (f32[48,1,1024]{2,0,1:T(8,128)S(1)}, f32[48,1,1024]{2,0,1:T(8,128)S(1)}, u32[]{:S(2)}, u32[]{:S(2)}) collective-permute-start(f32[48,1,1024]{2,0,1:T(8,128)S(1)} %get-tuple-element.34), channel_id=1, source_target_pairs={{0,1},{1,2},{2,3},{3,4},{4,5},{5,6},{6,7},{7,8},{8,9},{9,10},{10,1... | collective-permute-start | bytes 589832 | tf_op jit(solution)/shard_map/ppermute | solution.py:17
  8.2 7.0 %collective-permute-start = (f32[48,1,1024]{2,0,1:T(8,128)S(1)}, f32[48,1,1024]{2,0,1:T(8,128)S(1)}, u32[]{:S(2)}, u32[]{:S(2)}) collective-permute-start(f32[48,1,1024]{2,0,1:T(8,128)S(1)} %get-tuple-element.35), channel_id=1, source_target_pairs={{1,0},{2,1},{3,2},{4,3},{5,4},{6,5},{7,6},{8,7},{9,8},{10,9},{11,1... | collective-permute-start | bytes 589832 | tf_op jit(solution)/shard_map/ppermute | solution.py:19
  10.1 42.3 %copy-start.3 = (f32[8,1024]{1,0:T(8,128)}, f32[8,1024]{1,0:T(8,128)S(1)}, u32[]{:S(2)}) copy-start(f32[8,1024]{1,0:T(8,128)S(1)} %add_add_fusion) | copy-start | bytes 98308
  10.1 5.6 %copy-start.2 = (s32[48,8,1024]{2,1,0:T(8,128)S(1)}, s32[48,8,1024]{2,1,0:T(8,128)}, u32[]{:S(2)}) copy-start(s32[48,8,1024]{2,1,0:T(8,128)} %param.4) | copy-start | bytes 4718596
  39.3 2.6 %copy-start.13 = (f32[48]{0:T(128)}, f32[48]{0:T(128)S(1)}, u32[]{:S(2)}) copy-start(f32[48]{0:T(128)S(1)} %slice_divide_fusion.1) | copy-start | bytes 580
  42.0 5.4 %collective-permute-start.3 = (f32[48,1,1024]{2,0,1:T(8,128)S(1)}, f32[48,1,1024]{2,0,1:T(8,128)S(1)}, u32[]{:S(2)}, u32[]{:S(2)}) collective-permute-start(f32[48,1,1024]{2,0,1:T(8,128)S(1)} %get-tuple-element.32), channel_id=1, source_target_pairs={{0,1},{1,2},{2,3},{3,4},{4,5},{5,6},{6,7},{7,8},{8,9},{9,10},{10,1... | collective-permute-start | bytes 589832 | tf_op jit(solution)/shard_map/ppermute | solution.py:17
  44.8 7.0 %collective-permute-start.2 = (f32[48,1,1024]{2,0,1:T(8,128)S(1)}, f32[48,1,1024]{2,0,1:T(8,128)S(1)}, u32[]{:S(2)}, u32[]{:S(2)}) collective-permute-start(f32[48,1,1024]{2,0,1:T(8,128)S(1)} %get-tuple-element.33), channel_id=1, source_target_pairs={{1,0},{2,1},{3,2},{4,3},{5,4},{6,5},{7,6},{8,7},{9,8},{10,9},{11,1... | collective-permute-start | bytes 589832 | tf_op jit(solution)/shard_map/ppermute | solution.py:19
  74.9 5.4 %collective-permute-start.5 = (f32[48,1,1024]{2,0,1:T(8,128)S(1)}, f32[48,1,1024]{2,0,1:T(8,128)S(1)}, u32[]{:S(2)}, u32[]{:S(2)}) collective-permute-start(f32[48,1,1024]{2,0,1:T(8,128)S(1)} %get-tuple-element.30), channel_id=1, source_target_pairs={{0,1},{1,2},{2,3},{3,4},{4,5},{5,6},{6,7},{7,8},{8,9},{9,10},{10,1... | collective-permute-start | bytes 589832 | tf_op jit(solution)/shard_map/ppermute | solution.py:17
  77.7 7.6 %copy-start.4 = (f32[8,1024]{1,0:T(8,128)S(1)}, f32[8,1024]{1,0:T(8,128)}, u32[]{:S(2)}) copy-start(f32[8,1024]{1,0:T(8,128)} %copy-done.3) | copy-start | bytes 98308
  77.7 7.0 %collective-permute-start.4 = (f32[48,1,1024]{2,0,1:T(8,128)S(1)}, f32[48,1,1024]{2,0,1:T(8,128)S(1)}, u32[]{:S(2)}, u32[]{:S(2)}) collective-permute-start(f32[48,1,1024]{2,0,1:T(8,128)S(1)} %get-tuple-element.31), channel_id=1, source_target_pairs={{1,0},{2,1},{3,2},{4,3},{5,4},{6,5},{7,6},{8,7},{9,8},{10,9},{11,1... | collective-permute-start | bytes 589832 | tf_op jit(solution)/shard_map/ppermute | solution.py:19
  85.3 1.4 copy-start
  106.0 3.9 %copy-start.9 = (f32[48]{0:T(128)}, f32[48]{0:T(128)S(1)}, u32[]{:S(2)}) copy-start(f32[48]{0:T(128)S(1)} %get-tuple-element.20) | copy-start | bytes 580
  106.0 4.0 %copy-start.11 = (f32[48]{0:T(128)}, f32[48]{0:T(128)S(1)}, u32[]{:S(2)}) copy-start(f32[48]{0:T(128)S(1)} %get-tuple-element.22) | copy-start | bytes 580
  109.9 10.7 %copy-start.1 = (f32[48,8,1024]{2,0,1:T(8,128)}, f32[48,8,1024]{2,0,1:T(8,128)S(1)}, u32[]{:S(2)}) copy-start(f32[48,8,1024]{2,0,1:T(8,128)S(1)} %multiply_subtract_fusion) | copy-start | bytes 4718596
  110.0 5.6 %collective-permute-start.7 = (f32[48,1,1024]{2,0,1:T(8,128)S(1)}, f32[48,1,1024]{2,0,1:T(8,128)S(1)}, u32[]{:S(2)}, u32[]{:S(2)}) collective-permute-start(f32[48,1,1024]{2,0,1:T(8,128)S(1)} %get-tuple-element.28), channel_id=1, source_target_pairs={{0,1},{1,2},{2,3},{3,4},{4,5},{5,6},{6,7},{7,8},{8,9},{9,10},{10,1... | collective-permute-start | bytes 589832 | tf_op jit(solution)/shard_map/ppermute | solution.py:17
  113.0 7.7 %copy-start.5 = (f32[8,1024]{1,0:T(8,128)S(1)}, f32[8,1024]{1,0:T(8,128)}, u32[]{:S(2)}) copy-start(f32[8,1024]{1,0:T(8,128)} %copy-done.3) | copy-start | bytes 98308
  113.0 7.0 %collective-permute-start.6 = (f32[48,1,1024]{2,0,1:T(8,128)S(1)}, f32[48,1,1024]{2,0,1:T(8,128)S(1)}, u32[]{:S(2)}, u32[]{:S(2)}) collective-permute-start(f32[48,1,1024]{2,0,1:T(8,128)S(1)} %get-tuple-element.29), channel_id=1, source_target_pairs={{1,0},{2,1},{3,2},{4,3},{5,4},{6,5},{7,6},{8,7},{9,8},{10,9},{11,1... | collective-permute-start | bytes 589832 | tf_op jit(solution)/shard_map/ppermute | solution.py:19
  120.6 18.2 %copy-start.15 = (f32[48]{0:T(128)S(1)}, f32[48]{0:T(128)}, u32[]{:S(2)}) copy-start(f32[48]{0:T(128)} %get-tuple-element.21) | copy-start | bytes 580
  120.6 18.3 %copy-start.10 = (f32[48]{0:T(128)S(1)}, f32[48]{0:T(128)}, u32[]{:S(2)}) copy-start(f32[48]{0:T(128)} %copy-done.9) | copy-start | bytes 580
  120.7 18.3 %copy-start.12 = (f32[48]{0:T(128)S(1)}, f32[48]{0:T(128)}, u32[]{:S(2)}) copy-start(f32[48]{0:T(128)} %copy-done.11) | copy-start | bytes 580
  120.7 18.2 %copy-start.14 = (f32[48]{0:T(128)S(1)}, f32[48]{0:T(128)}, u32[]{:S(2)}) copy-start(f32[48]{0:T(128)} %copy-done.13) | copy-start | bytes 580
  145.2 14.1 %all-to-all-start.4 = ((f32[64,1,1]{2,1,0:T(1,128)}), f32[64,1,1]{2,1,0:T(1,128)S(1)}, u32[]{:S(2)}, u32[]{:S(2)}) async-start(f32[64,1,1]{2,1,0:T(1,128)} %broadcast_in_dim.16), calls=%async_computation.4 | async-start | bytes 65536 | tf_op jit(solution)/shard_map/all_to_all | solution.py:28
where the time goes:
time: 172 us; the launch traced here: 171 us
  blocking collectives  80.2 us (47%)
  other arithmetic  30 us (17%)
  waiting for transfers between devices  26.1 us (15%)
  starting transfers between devices  25.9 us (15%)
  local copies, waits for them, and re-layouts  6.18 us (4%)
  between operations  2.8 us (2%)
    all_to_all x5, blocking collectives, sent_to_all(): return lax.all_to_all(copies, axis, split_axis=0, concat_axis=0, tiled=True)  80.2 us
    ppermute x4, waiting for transfers between devices, with_halo(): lax.ppermute(head, axis, [((i + 1) % count, i) for i in range(ends)])  17.6 us
    ppermute x4, starting transfers between devices, with_halo(): lax.ppermute(tail, axis, [(i, (i + 1) % count) for i in range(ends)])  13.5 us
    sub x3, other arithmetic, on_device(): residual = residual - step_len[:, None, None] * applied_dir  9 us
    ppermute x4, starting transfers between devices, with_halo(): lax.ppermute(head, axis, [((i + 1) % count, i) for i in range(ends)])  7.68 us
    reduce_sum x4, other arithmetic, per_probe(): return jnp.sum(values, axis=(1, 2))  6.45 us
    all_to_all x1, waiting for transfers between devices, sent_to_all(): return lax.all_to_all(copies, axis, split_axis=0, concat_axis=0, tiled=True)  5.96 us
    reduce_sum x1, other arithmetic, on_device(): local_part = jnp.sum(probes * solution)  5.06 us
  transfers between devices with their start and end apart: 9, of which 9 were waited for; matrix products, arithmetic and copies ran while one was open for 2% of the time, Pallas kernels for 0%

commit v1 on v0

v1 whole, which is shorter than its diff:
```python
import functools

import jax
import jax.numpy as jnp
from jax import lax
from jax.experimental import pallas as pl
from jax.experimental.pallas import tpu as pltpu
from jax.sharding import PartitionSpec as P


ITERS = 4
SHIFT = 9.0
LANES = 128
GROUP = 8
CHUNKS = 2
AMPLIFIED = 600.0
VMEM_LIMIT = 16 * 1024 * 1024


VMEM = pl.BlockSpec(memory_space=pltpu.VMEM)
HBM = pl.BlockSpec(memory_space=pltpu.HBM)


def operate(vector, diagonal):
    strips = lax.axis_size("space")
    above = lax.ppermute(vector[:, -1:], "space", [(i, i + 1) for i in range(strips - 1)])
    below = lax.ppermute(vector[:, :1], "space", [(i + 1, i) for i in range(strips - 1)])
    padded = jnp.pad(jnp.concatenate([above, vector, below], axis=1), ((0, 0), (0, 0), (1, 1)))
    beside = padded[:, 2:, 1:-1] + padded[:, :-2, 1:-1]
    beside = beside + padded[:, 1:-1, 2:] + padded[:, 1:-1, :-2]
    return (4.0 + diagonal) * vector - beside


def of_everyone(values, axis):
    copies = jnp.broadcast_to(values, (lax.axis_size(axis), *values.shape))
    return jnp.sum(lax.all_to_all(copies, axis, split_axis=0, concat_axis=0, tiled=True), axis=0)


def per_probe(values):
    return of_everyone(jnp.sum(values, axis=(1, 2)), "space")


def iterate_on_device(probe_signs, diagonal):
    probes = 2.0 * probe_signs.astype(jnp.float32) - 1.0

    def iteration(_, state):
        solution, residual, direction, norm_now = state
        applied = operate(direction, diagonal)
        step = (norm_now / per_probe(direction * applied))[:, None, None]
        solution = solution + step * direction
        residual = residual - step * applied
        norm_next = per_probe(residual * residual)
        direction = residual + (norm_next / norm_now)[:, None, None] * direction
        return solution, residual, direction, norm_next

    cells = probes.shape[1] * lax.axis_size("space") * probes.shape[2]
    norm_now = jnp.full((probes.shape[0],), float(cells), jnp.float32)
    solution = lax.fori_loop(0, ITERS, iteration, (jnp.zeros_like(probes), probes, probes, norm_now))[0]
    quadratics = per_probe(probes * solution)
    trace_sum = of_everyone(jnp.sum(quadratics)[None], "probe")[0]
    return solution, trace_sum / float(probes.shape[0] * lax.axis_size("probe") * cells)


def edge_of(r, refs):
    up_ref, mid_ref, dn_ref = refs
    return (up_ref, r) if r < 4 else (mid_ref, 0) if r == 4 else (dn_ref, r - 5)


def prepare_kernel(signs_hbm, mask_hbm, weight_hbm, mass_hbm, *refs):
    outs = [refs[3 * n : 3 * n + 3] for n in range(CHUNKS)]
    signs_ref, mask_ref, weight_ref, mass_ref, sems = refs[3 * CHUNKS :]
    probes, rows, columns = signs_ref.shape
    count = probes // CHUNKS
    groups = probes // GROUP
    fields = [(mask_hbm, mask_ref), (weight_hbm, weight_ref), (mass_hbm, mass_ref)]
    copies = []
    for g in range(groups):
        mine = pl.ds(g * GROUP, GROUP)
        copies.append(pltpu.make_async_copy(signs_hbm.at[mine], signs_ref.at[mine], sems.at[g]))
    for n, (src, dst) in enumerate(fields):
        copies.append(pltpu.make_async_copy(src, dst, sems.at[groups + n]))
    for copy in copies:
        copy.start()
    for g in range(groups):
        copies[g].wait()
        refs = outs[g * GROUP // count]
        base = g * GROUP % count
        for c in range(columns // LANES):
            at = slice(c * LANES, (c + 1) * LANES)
            block = 2.0 * signs_ref[g * GROUP : (g + 1) * GROUP, :, at].astype(jnp.float32) - 1.0
            block = jnp.swapaxes(block, 0, 1)
            for r in range(rows):
                ref, start = edge_of(r, refs)
                ref[start * count + base : start * count + base + GROUP, at] = block[r]
    for copy in copies[groups:]:
        copy.wait()
    diagonal = mask_ref[...].astype(jnp.float32) * weight_ref[...] + mass_ref[...]
    outs[0][0][4 * count :, :] = diagonal
    outs[0][2][3 * count :, :] = diagonal


def powers_kernel(chunk, *refs):
    up_ref, mid_ref, dn_ref, below_ref, above_ref = refs[:5]
    if chunk:
        up_dd_ref, below_dd_ref, above_dd_ref, earlier_ref = refs[5:9]
        v1_ref, v2_ref, v3_ref, sums_ref, dd_ref, h1_ref, h2_ref, h3_ref, total_ref, part_ref = refs[9:]
    else:
        up_dd_ref, below_dd_ref, above_dd_ref = up_ref, below_ref, above_ref
        v1_ref, v2_ref, v3_ref, part_ref, dd_ref, h1_ref, h2_ref, h3_ref = refs[5:]
    rows, probes, columns = v1_ref.shape
    tiles = columns // LANES
    lane = lax.broadcasted_iota(jnp.int32, (GROUP, LANES), 1)
    first, last = lane == 0, lane == LANES - 1
    nothing = jnp.zeros((GROUP, LANES), jnp.float32)

    def at(c):
        return pl.ds(c * LANES, LANES)

    def spread(ref, row, to):
        line = ref[row : row + 1, :]
        dd_ref[to] = jnp.broadcast_to(line + (4.0 - SHIFT), (GROUP, columns))
        return jnp.where(jnp.broadcast_to(line[:, :LANES], (GROUP, LANES)) > 0.0, 1.0, 0.0)

    spread(above_dd_ref, 3 * probes + 6, 0)
    in_above = spread(above_dd_ref, 3 * probes + 7, 1)
    for r in range(rows):
        spread(up_dd_ref, 4 * probes + r, r + 2)
    in_below = spread(below_dd_ref, 4 * probes, 10)
    spread(below_dd_ref, 4 * probes + 1, 11)
    spread(below_dd_ref, 4 * probes + 2, 12)
    part_ref[7 * probes :, :] = jnp.zeros((probes, LANES), jnp.float32)

    own = [None, v1_ref, v2_ref, v3_ref]
    halo = [None, h1_ref, h2_ref, h3_ref]
    place = [None, {-2: 0, -1: 1, 8: 2, 9: 3, 10: 4}, {-1: 0, 8: 1, 9: 2}, {8: 0}]

    def where(level, r, base):
        if level:
            if 0 <= r < rows:
                return own[level], (r, pl.ds(base, GROUP))
            return halo[level], (place[level][r], slice(None))
        if r < 0:
            return above_ref, (pl.ds((r + 3) * probes + base, GROUP),)
        if r < 4:
            return up_ref, (pl.ds(r * probes + base, GROUP),)
        if r == 4:
            return mid_ref, (pl.ds(base, GROUP),)
        if r < rows:
            return dn_ref, (pl.ds((r - 5) * probes + base, GROUP),)
        return below_ref, (pl.ds((r - rows) * probes + base, GROUP),)

    def sideways(v):
        left = [pltpu.roll(t, 1, 1) for t in v]
        right = [pltpu.roll(t, LANES - 1, 1) for t in v]
        out = []
        for c in range(tiles):
            a = jnp.where(first, left[c - 1] if c else nothing, left[c])
            b = jnp.where(last, right[c + 1] if c + 1 < tiles else nothing, right[c])
            out.append(a + b)
        return out

    def group(g, carry):
        base = pl.multiple_of(g * GROUP, GROUP)

        def line(level, r):
            ref, index = where(level, r, base)
            return [ref[index + (at(c),)] for c in range(tiles)]

        totals = []
        for level, (begin, end) in enumerate([(-2, 11), (-1, 10), (0, 9)]):
            cross, square = nothing, nothing
            before, here = line(level, begin - 1), line(level, begin)
            for r in range(begin, end):
                after = line(level, r + 1)
                side = sideways(here)
                ref, index = where(level + 1, r, base)
                for c in range(tiles):
                    value = dd_ref[r + 2, :, at(c)] * here[c] - (side[c] + (before[c] + after[c]))
                    if r < 0:
                        value = in_above * value
                    if r >= rows:
                        value = in_below * value
                    ref[index + (at(c),)] = value
                    if 0 <= r < rows:
                        cross = cross + here[c] * value
                        square = square + value * value
                before, here = here, after
            totals += [cross, square]
        quad = nothing
        here = line(3, 0)
        for r in range(rows):
            after = line(3, r + 1)
            side = sideways(here)
            for c in range(tiles):
                quad = quad + here[c] * (dd_ref[r + 2, :, at(c)] * here[c] - (side[c] + (after[c] + after[c])))
            here = after
        totals.append(quad)
        for k, total in enumerate(totals):
            part_ref[pl.ds(k * probes + base, GROUP), :] = total
        return carry

    lax.fori_loop(0, probes // GROUP, group, 0)
    if not chunk:
        return
    for k in range(8):
        begin = k * CHUNKS * probes
        total_ref[begin : begin + probes, :] = earlier_ref[k * probes : (k + 1) * probes, :]
        total_ref[begin + probes : begin + 2 * probes, :] = part_ref[k * probes : (k + 1) * probes, :]
    ones = jnp.ones((GROUP, LANES), jnp.float32)
    line = lax.dot_general(
        ones, total_ref[...], (((1,), (1,)), ((), ())),
        precision=lax.Precision.HIGHEST, preferred_element_type=jnp.float32,
    )
    sums_ref[...] = jnp.broadcast_to(line[None, 0:1, :], sums_ref.shape)


def quadratic(c, moments):
    total = None
    n = len(c)
    for s in range(2 * n - 1):
        pairs = [c[a] * c[s - a] for a in range(max(0, s - n + 1), min(n, s + 1))]
        term = functools.reduce(lambda a, b: a + b, pairs) * moments[s]
        total = term if total is None else total + term
    return total


def coefficients(mu, shift):
    zero = jnp.zeros_like(mu[0])
    size = [jnp.abs(m) for m in mu]
    moved = [mu[k + 1] + shift * mu[k] for k in range(2 * ITERS - 1)]
    moved_size = [size[k + 1] + shift * size[k] for k in range(2 * ITERS - 1)]
    residual = [jnp.ones_like(mu[0])]
    direction = residual
    solution = [zero] * ITERS
    norm_now = mu[0]
    lost = jnp.ones_like(mu[0])
    amplified = zero
    for i in range(ITERS):
        curvature = quadratic(direction, moved)
        step = norm_now / curvature
        loss = quadratic([jnp.abs(d) for d in direction], moved_size) / jnp.abs(curvature)
        length = jnp.sqrt(jnp.abs(quadratic(direction, mu)))
        amplified = amplified + (loss + lost) * (jnp.abs(step) * length)
        solution = [x + step * direction[k] if k <= i else x for k, x in enumerate(solution)]
        if i + 1 < ITERS:
            applied = [shift * d for d in direction] + [zero]
            applied = [a + (direction[k - 1] if k else zero) for k, a in enumerate(applied)]
            residual = [r - step * a for r, a in zip(residual + [zero], applied)]
            norm_next = quadratic(residual, mu)
            lost = quadratic([jnp.abs(r) for r in residual], size) / jnp.abs(norm_next)
            ratio = norm_next / norm_now
            direction = [r + ratio * d for r, d in zip(residual, direction + [zero])]
            norm_now = norm_next
    for k in range(ITERS):
        amplified = amplified + jnp.abs(solution[k]) * jnp.sqrt(size[2 * k])
    length = jnp.sqrt(quadratic(solution, mu))
    return solution, amplified / length


def solve_kernel(cells, groups, sums_ref, coef_ref, trace_ref):
    row = jnp.sum(sums_ref[...], axis=0)
    width = row.shape[1]
    probes = width // 8
    row = jnp.broadcast_to(row, (8, width))
    mu = [jnp.full((8, LANES), cells, jnp.float32)]
    for k in range(2 * ITERS - 1):
        moved = pltpu.roll(row, width - k * probes, 1) if k else row
        mu.append(moved[:, :LANES])
    coef, amplified = coefficients(mu, SHIFT)
    sub = lax.broadcasted_iota(jnp.int32, (8, LANES), 0)
    lane = lax.broadcasted_iota(jnp.int32, (8, LANES), 1)
    packed = jnp.zeros((8, LANES), jnp.float32)
    trace = jnp.zeros((8, LANES), jnp.float32)
    for k in range(ITERS):
        packed = jnp.where(sub == k, coef[k], packed)
        trace = trace + coef[k] * mu[k]
    trace = jnp.where(lane < probes, trace, 0.0)
    total = jnp.sum(trace, axis=1, keepdims=True) / (float(probes * groups) * cells)
    unsafe = jnp.where(amplified < AMPLIFIED, 0.0, 1.0)
    unsafe = jnp.max(jnp.where(lane < probes, unsafe, 0.0), axis=1, keepdims=True)
    both = jnp.where(lane < LANES // 2, jnp.broadcast_to(total, lane.shape), jnp.broadcast_to(unsafe, lane.shape))
    trace_ref[...] = jnp.where(lane < LANES - 1, both, 0.0)[0:1]
    across = jnp.transpose(packed)
    for k in range(ITERS):
        coef_ref[k * probes : (k + 1) * probes, :] = jnp.broadcast_to(across[:probes, k : k + 1], (probes, LANES))


def combine_kernel(coef_ref, *refs):
    chunks = [refs[6 * n : 6 * n + 6] for n in range(CHUNKS)]
    out_ref, made_ref, sems = refs[6 * CHUNKS :]
    probes, rows, columns = made_ref.shape
    count = probes // CHUNKS

    def copy(g):
        mine = pl.ds(g * GROUP, GROUP)
        return pltpu.make_async_copy(made_ref.at[mine], out_ref.at[mine], sems.at[g])

    for g in range(probes // GROUP):
        v1_ref, v2_ref, v3_ref = chunks[g * GROUP // count][3:]
        base = g * GROUP
        local = base % count
        mine = slice(local, local + GROUP)
        c = [coef_ref[k * probes + base : k * probes + base + GROUP, :] for k in range(ITERS)]
        for t in range(columns // LANES):
            at = slice(t * LANES, (t + 1) * LANES)
            made = []
            for r in range(rows):
                ref, start = edge_of(r, chunks[base // count][:3])
                probe = ref[start * count + local : start * count + local + GROUP, at]
                made.append(
                    (c[0] * probe + c[1] * v1_ref[r, mine, at]) + (c[2] * v2_ref[r, mine, at] + c[3] * v3_ref[r, mine, at])
                )
            made_ref[base : base + GROUP, :, at] = jnp.swapaxes(jnp.stack(made), 0, 1)
        copy(g).start()
    for g in range(probes // GROUP):
        copy(g).wait()


def on_device(probe_signs, sensor_mask, sensor_weight, prior_mass):
    probes, rows, columns = probe_signs.shape
    strips = lax.axis_size("space")
    groups = lax.axis_size("probe")
    count = probes // CHUNKS
    params = pltpu.CompilerParams(vmem_limit_bytes=VMEM_LIMIT)

    def shaped(*shape):
        return jax.ShapeDtypeStruct(shape, jnp.float32)

    extra = [8] + [0] * (CHUNKS - 1)
    edges = pl.pallas_call(
        prepare_kernel,
        in_specs=[HBM] * 4,
        out_specs=[VMEM] * (3 * CHUNKS),
        out_shape=[shaped(r * count + (e if r > 1 else 0), columns) for e in extra for r in (4, 1, 3)],
        scratch_shapes=[
            pltpu.VMEM((probes, rows, columns), jnp.int32),
            pltpu.VMEM((rows, columns), jnp.int32),
            pltpu.VMEM((rows, columns), jnp.float32),
            pltpu.VMEM((rows, columns), jnp.float32),
            pltpu.SemaphoreType.DMA((probes // GROUP + 3,)),
        ],
        compiler_params=params,
    )(probe_signs, sensor_mask, sensor_weight, prior_mass)
    edges = [edges[3 * n : 3 * n + 3] for n in range(CHUNKS)]

    received = []
    for up, mid, dn in edges:
        below = lax.ppermute(up, "space", [(i + 1, i) for i in range(strips - 1)])
        above = lax.ppermute(dn, "space", [(i, i + 1) for i in range(strips - 1)])
        received.append((below, above))

    field = shaped(rows, count, columns)
    powers = []
    for n, ((up, mid, dn), (below, above)) in enumerate(zip(edges, received)):
        args = [up, mid, dn, below, above]
        sums = shaped(8 * count, LANES)
        scratch = [pltpu.VMEM((size, GROUP, columns), jnp.float32) for size in (rows + 5, 5, 3, 1)]
        if n:
            args += [edges[0][0], *received[0], powers[0][3]]
            sums = shaped(strips, 1, 8 * probes)
            scratch += [pltpu.VMEM((8 * probes, LANES), jnp.float32), pltpu.VMEM((8 * count, LANES), jnp.float32)]
        powers.append(
            pl.pallas_call(
                functools.partial(powers_kernel, n),
                in_specs=[VMEM] * len(args),
                out_specs=[VMEM] * 4,
                out_shape=[field, field, field, sums],
                scratch_shapes=scratch,
                compiler_params=params,
            )(*args)
        )

    sums = lax.all_to_all(powers[-1][3], "space", split_axis=0, concat_axis=0, tiled=True)

    cells = float(rows * strips * columns)
    coef, trace = pl.pallas_call(
        functools.partial(solve_kernel, cells, groups),
        in_specs=[VMEM],
        out_specs=[VMEM, VMEM],
        out_shape=[shaped(ITERS * probes, LANES), shaped(1, LANES)],
        compiler_params=params,
    )(sums)

    one, two, three = [
        lax.ppermute(trace, "probe", [(i, (i + k) % groups) for i in range(groups)])
        for k in range(1, groups)
    ]

    args = [coef]
    for edge, power in zip(edges, powers):
        args += [*edge, *power[:3]]
    combined = pl.pallas_call(
        combine_kernel,
        in_specs=[VMEM] * len(args),
        out_specs=HBM,
        out_shape=shaped(probes, rows, columns),
        scratch_shapes=[
            pltpu.VMEM((probes, rows, columns), jnp.float32),
            pltpu.SemaphoreType.DMA((probes // GROUP,)),
        ],
        compiler_params=params,
        cost_estimate=pl.CostEstimate(
            flops=8 * probes * rows * columns, bytes_accessed=20 * probes * rows * columns, transcendentals=0
        ),
    )(*args)

    everyone = (trace + two) + (one + three)

    def again(state):
        _, turn, _, _ = state
        past = turn.astype(jnp.int32)
        diagonal = (sensor_mask + past).astype(jnp.float32) * sensor_weight + prior_mass
        made, cell = iterate_on_device(probe_signs + past, diagonal)
        return turn, turn + 1.0, made, cell

    state = (everyone[0, LANES // 2], everyone[0, LANES - 1], combined, everyone[0, 0])
    return lax.while_loop(lambda state: state[0] > 0.0, again, state)[2:]


def solution(mesh):
    return jax.shard_map(
        on_device,
        mesh=mesh,
        in_specs=(P("probe", "space", None), P("space", None), P("space", None), P("space", None)),
        out_specs=(P("probe", "space", None), P()),
        check_vma=False,
    )
```

time: 172 us -> 54.2 us (0.32)
  blocking collectives: 80.2 us -> 21.9 us
  other arithmetic: 30 us -> 0.01 us
  waiting for transfers between devices: 26.1 us -> 2.88 us
  Pallas kernels: 0 us -> 8.48 us
  starting transfers between devices: 25.9 us -> 18.3 us
  local copies, waits for them, and re-layouts: 6.18 us -> 0.66 us
  between operations: 2.8 us -> 0.9 us
    all_to_all x5 -> x1, blocking collectives: 80.2 us -> 21.9 us  [on_device(): lax.all_to_all(powers[-1][3], 'space', split_axis=0, concat_axis=0, tiled...]
    ppermute x8 -> x7, waiting for transfers between devices: 20.2 us -> 2.88 us  [the longest x2 2.87 us: on_device(): above = lax.ppermute(dn, 'space', [(i, i + 1) for i in range(strips - 1)])]
    reduce_sum x11 -> x0, other arithmetic: 13.6 us -> none  [the longest x4 6.45 us: per_probe(): return jnp.sum(values, axis=(1, 2))]
    sub x4 -> x0, other arithmetic: 11.5 us -> none  [the longest x3 9 us: on_device(): residual = residual - step_len[:, None, None] * applied_dir]
    pallas_call x0 -> x5, Pallas kernels: none -> 8.48 us  [the longest x2 5.12 us: on_device(): pl.pallas_call(functools.partial(powers_kernel, n), in_specs=[VMEM] * len...]
    all_to_all x1 -> x0, waiting for transfers between devices: 5.96 us -> none  [sent_to_all(): return lax.all_to_all(copies, axis, split_axis=0, concat_axis=0, tiled=True)]
    all_to_all x1 -> x0, starting transfers between devices: 4.67 us -> none  [sent_to_all(): return lax.all_to_all(copies, axis, split_axis=0, concat_axis=0, tiled=True)]
    unnamed x33 -> x8, local copies, waits for them, and re-layouts: 4.07 us -> 0.01 us
  transfers between devices with their start and end apart: 9 -> 7, of which waited for: 9 -> 2; matrix products, arithmetic and copies ran while one was open for 2% -> 0% of each run, Pallas kernels for 0% -> 7%
where the time goes in v1:
time: 54.2 us; the launch traced here: 53.9 us
  blocking collectives  21.9 us (40%)
  starting transfers between devices  18.3 us (34%)
  Pallas kernels  8.48 us (16%)
  waiting for transfers between devices  2.88 us (5%)
  between operations  0.9 us (2%)
  loops' own time  0.81 us (1%)
  local copies, waits for them, and re-layouts  0.66 us (1%)
    all_to_all x1, blocking collectives, on_device(): lax.all_to_all(powers[-1][3], 'space', split_axis=0, concat_axis=0, tiled...  21.9 us
    ppermute x2, starting transfers between devices, on_device(): below = lax.ppermute(up, 'space', [(i + 1, i) for i in range(strips - 1)])  7.03 us
    ppermute x3, starting transfers between devices, on_device(): lax.ppermute(trace, 'probe', [(i, (i + k) % groups) for i in range(groups)])  5.67 us
    ppermute x2, starting transfers between devices, on_device(): above = lax.ppermute(dn, 'space', [(i, i + 1) for i in range(strips - 1)])  5.56 us
    pallas_call x2, Pallas kernels, on_device(): pl.pallas_call(functools.partial(powers_kernel, n), in_specs=[VMEM] * len...  5.12 us
    ppermute x2, waiting for transfers between devices, on_device(): above = lax.ppermute(dn, 'space', [(i, i + 1) for i in range(strips - 1)])  2.87 us
    pallas_call x1, Pallas kernels, on_device(): pl.pallas_call(prepare_kernel, in_specs=[HBM] * 4, out_specs=[VMEM] * (3...  1.51 us
    pallas_call x1, Pallas kernels, on_device(): pl.pallas_call(combine_kernel, in_specs=[VMEM] * len(args), out_specs=HBM...  1.43 us
  transfers between devices with their start and end apart: 7, of which 2 were waited for; matrix products, arithmetic and copies ran while one was open for 0% of the time, Pallas kernels for 7%

profile of v1, /device:TPU:1, one launch (start us, length us, event | category | flops | bytes accessed | tf_op | source)
XLA Modules:
  0.0 53.9 jit_solution(15992272011200308990)
XLA Ops:
  0.6 1.5 %shard_map.59 = (f32[104,1024]{1,0:T(8,128)S(1)}, f32[24,1024]{1,0:T(8,128)S(1)}, f32[80,1024]{1,0:T(8,128)S(1)}, f32[96,1024]{1,0:T(8,128)S(1)}, f32[24,1024]{1,0:T(8,128)S(1)}, /*index=5*/f32[72,1024]{1,0:T(8,128)S(1)}) custom-call(s32[48,8,1024]{2,1,0:T(8,128)} %signs_hbm.1, s32[8,1024]{1,0:T(8,128)} %mask_hbm.1, f32[8,1024]{1,0:T(8,128)} %weight_hbm.1, ...), custom_call_target="tpu_custom_call" | custom-call | tf_op jit(solution)/shard_map/pallas_call | solution.py:330
  2.1 5.1 %collective-permute-start.4 = (f32[104,1024]{1,0:T(8,128)S(1)}, f32[104,1024]{1,0:T(8,128)S(1)}, u32[]{:S(2)}, u32[]{:S(2)}) collective-permute-start(f32[104,1024]{1,0:T(8,128)S(1)} %get-tuple-element.220.refs_0_.refs_5_), channel_id=1, source_target_pairs={{1,0},{2,1},{3,2},{4,3},{5,4},{6,5},{7,6},{8,7},{9,8},{10,9},{11,1... | collective-permute-start | bytes 1277960 | tf_op jit(solution)/shard_map/ppermute | solution.py:348
  7.3 1.9 %collective-permute-start.2 = (f32[96,1024]{1,0:T(8,128)S(1)}, f32[96,1024]{1,0:T(8,128)S(1)}, u32[]{:S(2)}, u32[]{:S(2)}) collective-permute-start(f32[96,1024]{1,0:T(8,128)S(1)} %get-tuple-element.217.refs_0_.refs_6_), channel_id=1, source_target_pairs={{1,0},{2,1},{3,2},{4,3},{5,4},{6,5},{7,6},{8,7},{9,8},{10,9},{11,1... | collective-permute-start | bytes 1179656 | tf_op jit(solution)/shard_map/ppermute | solution.py:348
  9.2 3.6 %collective-permute-start.5 = (f32[80,1024]{1,0:T(8,128)S(1)}, f32[80,1024]{1,0:T(8,128)S(1)}, u32[]{:S(2)}, u32[]{:S(2)}) collective-permute-start(f32[80,1024]{1,0:T(8,128)S(1)} %get-tuple-element.221.refs_2_), channel_id=1, source_target_pairs={{0,1},{1,2},{2,3},{3,4},{4,5},{5,6},{6,7},{7,8},{8,9},{9,10},{10,1... | collective-permute-start | bytes 983048 | tf_op jit(solution)/shard_map/ppermute | solution.py:349
  12.8 1.9 %collective-permute-start.3 = (f32[72,1024]{1,0:T(8,128)S(1)}, f32[72,1024]{1,0:T(8,128)S(1)}, u32[]{:S(2)}, u32[]{:S(2)}) collective-permute-start(f32[72,1024]{1,0:T(8,128)S(1)} %get-tuple-element.219.refs_2_.refs_8_), channel_id=1, source_target_pairs={{0,1},{1,2},{2,3},{3,4},{4,5},{5,6},{6,7},{7,8},{8,9},{9,10},{10,1... | collective-permute-start | bytes 884744 | tf_op jit(solution)/shard_map/ppermute | solution.py:349
  14.8 2.1 %collective-permute-done.5.refs_4_.refs_7_ = f32[80,1024]{1,0:T(8,128)S(1)} collective-permute-done((f32[80,1024]{1,0:T(8,128)S(1)}, f32[80,1024]{1,0:T(8,128)S(1)}, u32[]{:S(2)}, u32[]{:S(2)}) %collective-permute-start.5) | collective-permute-done | bytes 327712 | tf_op jit(solution)/shard_map/ppermute | solution.py:349
  16.8 0.0 collective-permute-done.4.refs_3_.refs_6_
  16.8 2.3 %shard_map.60 = (f32[8,24,1024]{2,1,0:T(8,128)S(1)}, f32[8,24,1024]{2,1,0:T(8,128)S(1)}, f32[8,24,1024]{2,1,0:T(8,128)S(1)}, f32[192,128]{1,0:T(8,128)S(1)}) custom-call(f32[104,1024]{1,0:T(8,128)S(1)} %get-tuple-element.220.refs_0_.refs_5_, f32[24,1024]{1,0:T(8,128)S(1)} %get-tuple-element.222.refs_1_, f32[80,1024]{1,0:T(8,128)S(1)} %get-tuple-element.221.refs_2_, ...), custom_call_target="tpu_custom_call" | custom-call | tf_op jit(solution)/shard_map/pallas_call | solution.py:363
  19.2 0.8 %collective-permute-done.3.refs_4_ = f32[72,1024]{1,0:T(8,128)S(1)} collective-permute-done((f32[72,1024]{1,0:T(8,128)S(1)}, f32[72,1024]{1,0:T(8,128)S(1)}, u32[]{:S(2)}, u32[]{:S(2)}) %collective-permute-start.3) | collective-permute-done | bytes 294944 | tf_op jit(solution)/shard_map/ppermute | solution.py:349
  20.0 0.0 collective-permute-done.2.refs_3_
  20.0 2.8 %shard_map.61 = (f32[8,24,1024]{2,1,0:T(8,128)S(1)}, f32[8,24,1024]{2,1,0:T(8,128)S(1)}, f32[8,24,1024]{2,1,0:T(8,128)S(1)}, f32[64,1,384]{2,1,0:T(1,128)S(1)}) custom-call(f32[96,1024]{1,0:T(8,128)S(1)} %get-tuple-element.217.refs_0_.refs_6_, f32[24,1024]{1,0:T(8,128)S(1)} %get-tuple-element.218.refs_1_.refs_7_, ...), custom_call_target="tpu_custom_call" | custom-call | tf_op jit(solution)/shard_map/pallas_call | solution.py:363
  22.8 21.9 %all_to_all.49.sums_ref = f32[64,1,384]{2,1,0:T(1,128)S(1)} all-to-all(f32[64,1,384]{2,1,0:T(1,128)S(1)} %get-tuple-element.224), channel_id=1, replica_groups=mesh['probe'=4,'space'=64] {'space'}, dimensions={0} | all-to-all | bytes 196608 | tf_op jit(solution)/shard_map/all_to_all | solution.py:373
  44.7 0.4 shard_map.62
  45.1 3.0 %collective-permute-start.6 = (f32[1,128]{1,0:T(1,128)S(1)}, f32[1,128]{1,0:T(1,128)S(1)}, u32[]{:S(2)}, u32[]{:S(2)}) collective-permute-start(f32[1,128]{1,0:T(1,128)S(1)} %get-tuple-element.225), channel_id=1, source_target_pairs={{0,128},{64,192},{128,0},{192,64},{1,129},{65,193},{129,1},{193,65... | collective-permute-start | bytes 1544 | tf_op jit(solution)/shard_map/ppermute | solution.py:385
  48.1 0.4 collective-permute-start.7
  48.5 2.3 %collective-permute-start.8 = (f32[1,128]{1,0:T(1,128)S(1)}, f32[1,128]{1,0:T(1,128)S(1)}, u32[]{:S(2)}, u32[]{:S(2)}) collective-permute-start(f32[1,128]{1,0:T(1,128)S(1)} %get-tuple-element.225), channel_id=1, source_target_pairs={{0,192},{64,0},{128,64},{192,128},{1,193},{65,1},{129,65},{193,129... | collective-permute-start | bytes 1544 | tf_op jit(solution)/shard_map/ppermute | solution.py:385
  50.8 0.0 copy-start.1
  50.8 0.0 copy-start.4
  50.8 0.0 copy-start.6
  50.8 0.0 copy-start.8
  50.8 1.4 %shard_map.63 = f32[48,8,1024]{2,1,0:T(8,128)} custom-call(f32[192,128]{1,0:T(8,128)S(1)} %get-tuple-element.226.coef_ref, f32[104,1024]{1,0:T(8,128)S(1)} %get-tuple-element.220.refs_0_.refs_5_, f32[24,1024]{1,0:T(8,128)S(1)} %get-tuple-element.222.refs_1_, f32[80,1024]{1,0:T(8,128)S(1)} %get-tuple-element.221.refs_2_, ...), custom_call_target="tpu_custom_call" | custom-call | flops 3145728 | bytes 7864320 | tf_op jit(solution)/shard_map/pallas_call | solution.py:392
  52.3 0.0 collective-permute-done.6
  52.3 0.0 collective-permute-done.7
  52.3 0.0 collective-permute-done.8
  52.3 0.6 %fusion.4 = (f32[1,1]{1,0:T(1,128)}, f32[1,1]{1,0:T(1,128)}, f32[1,1]{1,0:T(1,128)}) fusion(f32[1,128]{1,0:T(1,128)S(1)} %add_add_fusion), kind=kLoop, calls=%fused_computation.22 | loop fusion | bytes 24 | tf_op jit(solution)/shard_map/slice | solution.py:416
  53.0 0.0 copy-done.1
  53.0 0.0 copy-done.4
  53.0 0.0 copy-done.6
  53.0 0.0 copy-done.8
  53.0 0.8 %while.42 = (f32[]{:T(128)}, f32[]{:T(128)}, f32[48,8,1024]{2,1,0:T(8,128)}, f32[]{:T(128)}, s32[48,8,1024]{2,1,0:T(8,128)S(1)}, /*index=5*/s32[8,1024]{1,0:T(8,...) while((f32[]{:T(128)}, f32[]{:T(128)}, ...), condition=%wide.region_10.0_spmd, body=%wide.region_0.10_spmd.sunk | while | flops 17752440 | bytes 52235400 | solution.py:417
  (1 shorter events, 0.0 us)
Async XLA Ops:
  2.1 14.7 %collective-permute-start.4 = (f32[104,1024]{1,0:T(8,128)S(1)}, f32[104,1024]{1,0:T(8,128)S(1)}, u32[]{:S(2)}, u32[]{:S(2)}) collective-permute-start(f32[104,1024]{1,0:T(8,128)S(1)} %get-tuple-element.220.refs_0_.refs_5_), channel_id=1, source_target_pairs={{1,0},{2,1},{3,2},{4,3},{5,4},{6,5},{7,6},{8,7},{9,8},{10,9},{11,1... | collective-permute-start | bytes 1277960 | tf_op jit(solution)/shard_map/ppermute | solution.py:348
  7.3 12.7 %collective-permute-start.2 = (f32[96,1024]{1,0:T(8,128)S(1)}, f32[96,1024]{1,0:T(8,128)S(1)}, u32[]{:S(2)}, u32[]{:S(2)}) collective-permute-start(f32[96,1024]{1,0:T(8,128)S(1)} %get-tuple-element.217.refs_0_.refs_6_), channel_id=1, source_target_pairs={{1,0},{2,1},{3,2},{4,3},{5,4},{6,5},{7,6},{8,7},{9,8},{10,9},{11,1... | collective-permute-start | bytes 1179656 | tf_op jit(solution)/shard_map/ppermute | solution.py:348
  9.2 7.6 %collective-permute-start.5 = (f32[80,1024]{1,0:T(8,128)S(1)}, f32[80,1024]{1,0:T(8,128)S(1)}, u32[]{:S(2)}, u32[]{:S(2)}) collective-permute-start(f32[80,1024]{1,0:T(8,128)S(1)} %get-tuple-element.221.refs_2_), channel_id=1, source_target_pairs={{0,1},{1,2},{2,3},{3,4},{4,5},{5,6},{6,7},{7,8},{8,9},{9,10},{10,1... | collective-permute-start | bytes 983048 | tf_op jit(solution)/shard_map/ppermute | solution.py:349
  12.8 7.2 %collective-permute-start.3 = (f32[72,1024]{1,0:T(8,128)S(1)}, f32[72,1024]{1,0:T(8,128)S(1)}, u32[]{:S(2)}, u32[]{:S(2)}) collective-permute-start(f32[72,1024]{1,0:T(8,128)S(1)} %get-tuple-element.219.refs_2_.refs_8_), channel_id=1, source_target_pairs={{0,1},{1,2},{2,3},{3,4},{4,5},{5,6},{6,7},{7,8},{8,9},{9,10},{10,1... | collective-permute-start | bytes 884744 | tf_op jit(solution)/shard_map/ppermute | solution.py:349
  45.1 7.1 %collective-permute-start.6 = (f32[1,128]{1,0:T(1,128)S(1)}, f32[1,128]{1,0:T(1,128)S(1)}, u32[]{:S(2)}, u32[]{:S(2)}) collective-permute-start(f32[1,128]{1,0:T(1,128)S(1)} %get-tuple-element.225), channel_id=1, source_target_pairs={{0,128},{64,192},{128,0},{192,64},{1,129},{65,193},{129,1},{193,65... | collective-permute-start | bytes 1544 | tf_op jit(solution)/shard_map/ppermute | solution.py:385
  48.1 4.1 %collective-permute-start.7 = (f32[1,128]{1,0:T(1,128)S(1)}, f32[1,128]{1,0:T(1,128)S(1)}, u32[]{:S(2)}, u32[]{:S(2)}) collective-permute-start(f32[1,128]{1,0:T(1,128)S(1)} %get-tuple-element.225), channel_id=1, source_target_pairs={{0,64},{64,128},{128,192},{192,0},{1,65},{65,129},{129,193},{193,1... | collective-permute-start | bytes 1544 | tf_op jit(solution)/shard_map/ppermute | solution.py:385
  48.5 3.8 %collective-permute-start.8 = (f32[1,128]{1,0:T(1,128)S(1)}, f32[1,128]{1,0:T(1,128)S(1)}, u32[]{:S(2)}, u32[]{:S(2)}) collective-permute-start(f32[1,128]{1,0:T(1,128)S(1)} %get-tuple-element.225), channel_id=1, source_target_pairs={{0,192},{64,0},{128,64},{192,128},{1,193},{65,1},{129,65},{193,129... | collective-permute-start | bytes 1544 | tf_op jit(solution)/shard_map/ppermute | solution.py:385
  50.8 2.1 %copy-start.1 = (s32[48,8,1024]{2,1,0:T(8,128)S(1)}, s32[48,8,1024]{2,1,0:T(8,128)}, u32[]{:S(2)}) copy-start(s32[48,8,1024]{2,1,0:T(8,128)} %signs_hbm.1) | copy-start | bytes 4718596
  50.8 2.1 %copy-start.4 = (s32[8,1024]{1,0:T(8,128)S(1)}, s32[8,1024]{1,0:T(8,128)}, u32[]{:S(2)}) copy-start(s32[8,1024]{1,0:T(8,128)} %mask_hbm.1) | copy-start | bytes 98308
  50.8 2.1 %copy-start.6 = (f32[8,1024]{1,0:T(8,128)S(1)}, f32[8,1024]{1,0:T(8,128)}, u32[]{:S(2)}) copy-start(f32[8,1024]{1,0:T(8,128)} %weight_hbm.1) | copy-start | bytes 98308
  50.8 2.1 %copy-start.8 = (f32[8,1024]{1,0:T(8,128)S(1)}, f32[8,1024]{1,0:T(8,128)}, u32[]{:S(2)}) copy-start(f32[8,1024]{1,0:T(8,128)} %mass_hbm.1) | copy-start | bytes 98308

commit v2 on v1

--- a/solution.py
+++ b/solution.py
@@ -61,14 +61,18 @@
     return solution, trace_sum / float(probes.shape[0] * lax.axis_size("probe") * cells)
 
 
-def edge_of(r, refs):
-    up_ref, mid_ref, dn_ref = refs
-    return (up_ref, r) if r < 4 else (mid_ref, 0) if r == 4 else (dn_ref, r - 5)
+def edge_of(r, n, count, refs):
+    up_ref, mid_ref, *dn_refs = refs
+    if r < 4:
+        return up_ref, (r * CHUNKS + n) * count
+    if r == 4:
+        return mid_ref, n * count
+    return dn_refs[n], (r - 5) * count
 
 
 def prepare_kernel(signs_hbm, mask_hbm, weight_hbm, mass_hbm, *refs):
-    outs = [refs[3 * n : 3 * n + 3] for n in range(CHUNKS)]
-    signs_ref, mask_ref, weight_ref, mass_ref, sems = refs[3 * CHUNKS :]
+    outs = refs[: CHUNKS + 2]
+    signs_ref, mask_ref, weight_ref, mass_ref, sems = refs[CHUNKS + 2 :]
     probes, rows, columns = signs_ref.shape
     count = probes // CHUNKS
     groups = probes // GROUP
@@ -83,29 +87,28 @@
         copy.start()
     for g in range(groups):
         copies[g].wait()
-        refs = outs[g * GROUP // count]
-        base = g * GROUP % count
+        chunk, base = divmod(g * GROUP, count)
         for c in range(columns // LANES):
             at = slice(c * LANES, (c + 1) * LANES)
             block = 2.0 * signs_ref[g * GROUP : (g + 1) * GROUP, :, at].astype(jnp.float32) - 1.0
             block = jnp.swapaxes(block, 0, 1)
             for r in range(rows):
-                ref, start = edge_of(r, refs)
-                ref[start * count + base : start * count + base + GROUP, at] = block[r]
+                ref, start = edge_of(r, chunk, count, outs)
+                ref[start + base : start + base + GROUP, at] = block[r]
     for copy in copies[groups:]:
         copy.wait()
     diagonal = mask_ref[...].astype(jnp.float32) * weight_ref[...] + mass_ref[...]
-    outs[0][0][4 * count :, :] = diagonal
-    outs[0][2][3 * count :, :] = diagonal
+    outs[0][4 * probes :, :] = diagonal
+    outs[2][3 * count :, :] = diagonal
 
 
 def powers_kernel(chunk, *refs):
-    up_ref, mid_ref, dn_ref, below_ref, above_ref = refs[:5]
+    up_ref, mid_ref, below_ref, dn_ref, above_ref = refs[:5]
     if chunk:
-        up_dd_ref, below_dd_ref, above_dd_ref, earlier_ref = refs[5:9]
-        v1_ref, v2_ref, v3_ref, sums_ref, dd_ref, h1_ref, h2_ref, h3_ref, total_ref, part_ref = refs[9:]
+        above_dd_ref, earlier_ref = refs[5:7]
+        v1_ref, v2_ref, v3_ref, sums_ref, dd_ref, h1_ref, h2_ref, h3_ref, total_ref, part_ref = refs[7:]
     else:
-        up_dd_ref, below_dd_ref, above_dd_ref = up_ref, below_ref, above_ref
+        above_dd_ref = above_ref
         v1_ref, v2_ref, v3_ref, part_ref, dd_ref, h1_ref, h2_ref, h3_ref = refs[5:]
     rows, probes, columns = v1_ref.shape
     tiles = columns // LANES
@@ -124,10 +127,10 @@
     spread(above_dd_ref, 3 * probes + 6, 0)
     in_above = spread(above_dd_ref, 3 * probes + 7, 1)
     for r in range(rows):
-        spread(up_dd_ref, 4 * probes + r, r + 2)
-    in_below = spread(below_dd_ref, 4 * probes, 10)
-    spread(below_dd_ref, 4 * probes + 1, 11)
-    spread(below_dd_ref, 4 * probes + 2, 12)
+        spread(up_ref, 4 * CHUNKS * probes + r, r + 2)
+    in_below = spread(below_ref, 4 * CHUNKS * probes, 10)
+    spread(below_ref, 4 * CHUNKS * probes + 1, 11)
+    spread(below_ref, 4 * CHUNKS * probes + 2, 12)
     part_ref[7 * probes :, :] = jnp.zeros((probes, LANES), jnp.float32)
 
     own = [None, v1_ref, v2_ref, v3_ref]
@@ -142,12 +145,12 @@
         if r < 0:
             return above_ref, (pl.ds((r + 3) * probes + base, GROUP),)
         if r < 4:
-            return up_ref, (pl.ds(r * probes + base, GROUP),)
+            return up_ref, (pl.ds((r * CHUNKS + chunk) * probes + base, GROUP),)
         if r == 4:
-            return mid_ref, (pl.ds(base, GROUP),)
+            return mid_ref, (pl.ds(chunk * probes + base, GROUP),)
         if r < rows:
             return dn_ref, (pl.ds((r - 5) * probes + base, GROUP),)
-        return below_ref, (pl.ds((r - rows) * probes + base, GROUP),)
+        return below_ref, (pl.ds(((r - rows) * CHUNKS + chunk) * probes + base, GROUP),)
 
     def sideways(v):
         left = [pltpu.roll(t, 1, 1) for t in v]
@@ -286,8 +289,9 @@
 
 
 def combine_kernel(coef_ref, *refs):
-    chunks = [refs[6 * n : 6 * n + 6] for n in range(CHUNKS)]
-    out_ref, made_ref, sems = refs[6 * CHUNKS :]
+    edges = refs[: CHUNKS + 2]
+    powers = [refs[CHUNKS + 2 + 3 * n : CHUNKS + 5 + 3 * n] for n in range(CHUNKS)]
+    out_ref, made_ref, sems = refs[4 * CHUNKS + 2 :]
     probes, rows, columns = made_ref.shape
     count = probes // CHUNKS
 
@@ -296,17 +300,17 @@
         return pltpu.make_async_copy(made_ref.at[mine], out_ref.at[mine], sems.at[g])
 
     for g in range(probes // GROUP):
-        v1_ref, v2_ref, v3_ref = chunks[g * GROUP // count][3:]
         base = g * GROUP
-        local = base % count
+        chunk, local = divmod(base, count)
+        v1_ref, v2_ref, v3_ref = powers[chunk]
         mine = slice(local, local + GROUP)
         c = [coef_ref[k * probes + base : k * probes + base + GROUP, :] for k in range(ITERS)]
         for t in range(columns // LANES):
             at = slice(t * LANES, (t + 1) * LANES)
             made = []
             for r in range(rows):
-                ref, start = edge_of(r, chunks[base // count][:3])
-                probe = ref[start * count + local : start * count + local + GROUP, at]
+                ref, start = edge_of(r, chunk, count, edges)
+                probe = ref[start + local : start + local + GROUP, at]
                 made.append(
                     (c[0] * probe + c[1] * v1_ref[r, mine, at]) + (c[2] * v2_ref[r, mine, at] + c[3] * v3_ref[r, mine, at])
                 )
@@ -326,12 +330,12 @@
     def shaped(*shape):
         return jax.ShapeDtypeStruct(shape, jnp.float32)
 
-    extra = [8] + [0] * (CHUNKS - 1)
     edges = pl.pallas_call(
         prepare_kernel,
         in_specs=[HBM] * 4,
-        out_specs=[VMEM] * (3 * CHUNKS),
-        out_shape=[shaped(r * count + (e if r > 1 else 0), columns) for e in extra for r in (4, 1, 3)],
+        out_specs=[VMEM] * (CHUNKS + 2),
+        out_shape=[shaped(4 * probes + rows, columns), shaped(probes, columns)]
+        + [shaped(3 * count + (0 if n else rows), columns) for n in range(CHUNKS)],
         scratch_shapes=[
             pltpu.VMEM((probes, rows, columns), jnp.int32),
             pltpu.VMEM((rows, columns), jnp.int32),
@@ -341,22 +345,20 @@
         ],
         compiler_params=params,
     )(probe_signs, sensor_mask, sensor_weight, prior_mass)
-    edges = [edges[3 * n : 3 * n + 3] for n in range(CHUNKS)]
-
-    received = []
-    for up, mid, dn in edges:
-        below = lax.ppermute(up, "space", [(i + 1, i) for i in range(strips - 1)])
-        above = lax.ppermute(dn, "space", [(i, i + 1) for i in range(strips - 1)])
-        received.append((below, above))
+    up, mid, *downs = edges
+    below = lax.ppermute(up, "space", [(i + 1, i) for i in range(strips - 1)])
+    above = []
+    for dn in downs:
+        above.append(lax.ppermute(dn, "space", [(i, i + 1) for i in range(strips - 1)]))
 
     field = shaped(rows, count, columns)
     powers = []
-    for n, ((up, mid, dn), (below, above)) in enumerate(zip(edges, received)):
-        args = [up, mid, dn, below, above]
+    for n in range(CHUNKS):
+        args = [up, mid, below, downs[n], above[n]]
         sums = shaped(8 * count, LANES)
         scratch = [pltpu.VMEM((size, GROUP, columns), jnp.float32) for size in (rows + 5, 5, 3, 1)]
         if n:
-            args += [edges[0][0], *received[0], powers[0][3]]
+            args += [above[0], powers[0][3]]
             sums = shaped(strips, 1, 8 * probes)
             scratch += [pltpu.VMEM((8 * probes, LANES), jnp.float32), pltpu.VMEM((8 * count, LANES), jnp.float32)]
         powers.append(
@@ -386,9 +388,9 @@
         for k in range(1, groups)
     ]
 
-    args = [coef]
-    for edge, power in zip(edges, powers):
-        args += [*edge, *power[:3]]
+    args = [coef, *edges]
+    for power in powers:
+        args += power[:3]
     combined = pl.pallas_call(
         combine_kernel,
         in_specs=[VMEM] * len(args),

time: 54.2 us -> 53.7 us (level)
  starting transfers between devices: 18.3 us -> 14.9 us
  waiting for transfers between devices: 2.88 us -> 5.68 us
    ppermute x2 -> x1, waiting for transfers between devices: 0.01 us -> 3.9 us  [on_device(): below = lax.ppermute(up, 'space', [(i + 1, i) for i in range(strips - 1)])]
    ppermute x2 -> x1, starting transfers between devices: 7.03 us -> 5.11 us  [on_device(): below = lax.ppermute(up, 'space', [(i + 1, i) for i in range(strips - 1)])]
    ppermute x2, starting transfers between devices: 5.56 us -> 4.14 us  [on_device(): lax.ppermute(dn, 'space', [(i, i + 1) for i in range(strips - 1)])]
    ppermute x2, waiting for transfers between devices: 2.87 us -> 1.77 us  [on_device(): lax.ppermute(dn, 'space', [(i, i + 1) for i in range(strips - 1)])]
  transfers between devices with their start and end apart: 7 -> 6, of which waited for: 2 -> 2; matrix products, arithmetic and copies ran while one was open for 0% -> 0% of each run, Pallas kernels for 7% -> 7%
where the time goes in v2:
time: 53.7 us; the launch traced here: 53.4 us
  blocking collectives  21.9 us (41%)
  starting transfers between devices  14.9 us (28%)
  Pallas kernels  8.57 us (16%)
  waiting for transfers between devices  5.68 us (11%)
  between operations  0.9 us (2%)
  loops' own time  0.82 us (2%)
  local copies, waits for them, and re-layouts  0.63 us (1%)
    all_to_all x1, blocking collectives, on_device(): lax.all_to_all(powers[-1][3], 'space', split_axis=0, concat_axis=0, tiled...  21.9 us
    ppermute x3, starting transfers between devices, on_device(): lax.ppermute(trace, 'probe', [(i, (i + k) % groups) for i in range(groups)])  5.67 us
    pallas_call x2, Pallas kernels, on_device(): pl.pallas_call(functools.partial(powers_kernel, n), in_specs=[VMEM] * len...  5.2 us
    ppermute x1, starting transfers between devices, on_device(): below = lax.ppermute(up, 'space', [(i + 1, i) for i in range(strips - 1)])  5.11 us
    ppermute x2, starting transfers between devices, on_device(): lax.ppermute(dn, 'space', [(i, i + 1) for i in range(strips - 1)])  4.14 us
    ppermute x1, waiting for transfers between devices, on_device(): below = lax.ppermute(up, 'space', [(i + 1, i) for i in range(strips - 1)])  3.9 us
    ppermute x2, waiting for transfers between devices, on_device(): lax.ppermute(dn, 'space', [(i, i + 1) for i in range(strips - 1)])  1.77 us
    pallas_call x1, Pallas kernels, on_device(): pl.pallas_call(prepare_kernel, in_specs=[HBM] * 4, out_specs=[VMEM] * (CH...  1.51 us
  transfers between devices with their start and end apart: 6, of which 2 were waited for; matrix products, arithmetic and copies ran while one was open for 0% of the time, Pallas kernels for 7%

profile of v2, /device:TPU:1, one launch (start us, length us, event | category | flops | bytes accessed | tf_op | source)
XLA Modules:
  0.0 53.4 jit_solution(1486970609943678358)
XLA Ops:
  0.6 1.5 %shard_map.59 = (f32[200,1024]{1,0:T(8,128)S(1)}, f32[48,1024]{1,0:T(8,128)S(1)}, f32[80,1024]{1,0:T(8,128)S(1)}, f32[72,1024]{1,0:T(8,128)S(1)}) custom-call(s32[48,8,1024]{2,1,0:T(8,128)} %signs_hbm.1, s32[8,1024]{1,0:T(8,128)} %mask_hbm.1, f32[8,1024]{1,0:T(8,128)} %weight_hbm.1, f32[8,1024]{1,0:T(8,128)} %mass_hbm.1), custom_call_target="tpu_custom_call" | custom-call | tf_op jit(solution)/shard_map/pallas_call | solution.py:333
  2.1 5.1 %collective-permute-start.2 = (f32[200,1024]{1,0:T(8,128)S(1)}, f32[200,1024]{1,0:T(8,128)S(1)}, u32[]{:S(2)}, u32[]{:S(2)}) collective-permute-start(f32[200,1024]{1,0:T(8,128)S(1)} %get-tuple-element.215.refs_0_), channel_id=1, source_target_pairs={{1,0},{2,1},{3,2},{4,3},{5,4},{6,5},{7,6},{8,7},{9,8},{10,9},{11,1... | collective-permute-start | bytes 2457608 | tf_op jit(solution)/shard_map/ppermute | solution.py:349
  7.3 1.9 %collective-permute-start.4 = (f32[80,1024]{1,0:T(8,128)S(1)}, f32[80,1024]{1,0:T(8,128)S(1)}, u32[]{:S(2)}, u32[]{:S(2)}) collective-permute-start(f32[80,1024]{1,0:T(8,128)S(1)} %get-tuple-element.218.refs_3_.refs_2_), channel_id=1, source_target_pairs={{0,1},{1,2},{2,3},{3,4},{4,5},{5,6},{6,7},{7,8},{8,9},{9,10},{10,1... | collective-permute-start | bytes 983048 | tf_op jit(solution)/shard_map/ppermute | solution.py:352
  9.2 2.2 %collective-permute-start.3 = (f32[72,1024]{1,0:T(8,128)S(1)}, f32[72,1024]{1,0:T(8,128)S(1)}, u32[]{:S(2)}, u32[]{:S(2)}) collective-permute-start(f32[72,1024]{1,0:T(8,128)S(1)} %get-tuple-element.217.refs_3_), channel_id=1, source_target_pairs={{0,1},{1,2},{2,3},{3,4},{4,5},{5,6},{6,7},{7,8},{8,9},{9,10},{10,1... | collective-permute-start | bytes 884744 | tf_op jit(solution)/shard_map/ppermute | solution.py:352
  11.4 1.8 %collective-permute-done.4.refs_4_.refs_5_ = f32[80,1024]{1,0:T(8,128)S(1)} collective-permute-done((f32[80,1024]{1,0:T(8,128)S(1)}, f32[80,1024]{1,0:T(8,128)S(1)}, u32[]{:S(2)}, u32[]{:S(2)}) %collective-permute-start.4) | collective-permute-done | bytes 327712 | tf_op jit(solution)/shard_map/ppermute | solution.py:352
  13.2 3.9 %collective-permute-done.2.refs_2_ = f32[200,1024]{1,0:T(8,128)S(1)} collective-permute-done((f32[200,1024]{1,0:T(8,128)S(1)}, f32[200,1024]{1,0:T(8,128)S(1)}, u32[]{:S(2)}, u32[]{:S(2)}) %collective-permute-start.2) | collective-permute-done | bytes 819232 | tf_op jit(solution)/shard_map/ppermute | solution.py:349
  17.1 2.4 %shard_map.60 = (f32[8,24,1024]{2,1,0:T(8,128)S(1)}, f32[8,24,1024]{2,1,0:T(8,128)S(1)}, f32[8,24,1024]{2,1,0:T(8,128)S(1)}, f32[192,128]{1,0:T(8,128)S(1)}) custom-call(f32[200,1024]{1,0:T(8,128)S(1)} %get-tuple-element.215.refs_0_, f32[48,1024]{1,0:T(8,128)S(1)} %get-tuple-element.216.refs_1_, f32[200,1024]{1,0:T(8,128)S(1)} %collective-permute-done.2.refs_2_, ...), custom_call_target="tpu_custom_call" | custom-call | tf_op jit(solution)/shard_map/pallas_call | solution.py:365
  19.5 0.0 collective-permute-done.3.refs_4_
  19.5 2.8 %shard_map.61 = (f32[8,24,1024]{2,1,0:T(8,128)S(1)}, f32[8,24,1024]{2,1,0:T(8,128)S(1)}, f32[8,24,1024]{2,1,0:T(8,128)S(1)}, f32[64,1,384]{2,1,0:T(1,128)S(1)}) custom-call(f32[200,1024]{1,0:T(8,128)S(1)} %get-tuple-element.215.refs_0_, f32[48,1024]{1,0:T(8,128)S(1)} %get-tuple-element.216.refs_1_, f32[200,1024]{1,0:T(8,128)S(1)} %collective-permute-done.2.refs_2_, ...), custom_call_target="tpu_custom_call" | custom-call | tf_op jit(solution)/shard_map/pallas_call | solution.py:365
  22.3 21.9 %all_to_all.49.sums_ref = f32[64,1,384]{2,1,0:T(1,128)S(1)} all-to-all(f32[64,1,384]{2,1,0:T(1,128)S(1)} %get-tuple-element.220), channel_id=1, replica_groups=mesh['probe'=4,'space'=64] {'space'}, dimensions={0} | all-to-all | bytes 196608 | tf_op jit(solution)/shard_map/all_to_all | solution.py:375
  44.2 0.4 shard_map.62
  44.6 3.0 %collective-permute-start.5 = (f32[1,128]{1,0:T(1,128)S(1)}, f32[1,128]{1,0:T(1,128)S(1)}, u32[]{:S(2)}, u32[]{:S(2)}) collective-permute-start(f32[1,128]{1,0:T(1,128)S(1)} %get-tuple-element.221), channel_id=1, source_target_pairs={{0,128},{64,192},{128,0},{192,64},{1,129},{65,193},{129,1},{193,65... | collective-permute-start | bytes 1544 | tf_op jit(solution)/shard_map/ppermute | solution.py:387
  47.6 0.4 collective-permute-start.6
  48.0 2.3 %collective-permute-start.7 = (f32[1,128]{1,0:T(1,128)S(1)}, f32[1,128]{1,0:T(1,128)S(1)}, u32[]{:S(2)}, u32[]{:S(2)}) collective-permute-start(f32[1,128]{1,0:T(1,128)S(1)} %get-tuple-element.221), channel_id=1, source_target_pairs={{0,192},{64,0},{128,64},{192,128},{1,193},{65,1},{129,65},{193,129... | collective-permute-start | bytes 1544 | tf_op jit(solution)/shard_map/ppermute | solution.py:387
  50.3 0.0 copy-start.1
  50.3 0.0 copy-start.4
  50.3 0.0 copy-start.6
  50.3 0.0 copy-start.8
  50.3 1.4 %shard_map.63 = f32[48,8,1024]{2,1,0:T(8,128)} custom-call(f32[192,128]{1,0:T(8,128)S(1)} %get-tuple-element.222.coef_ref, f32[200,1024]{1,0:T(8,128)S(1)} %get-tuple-element.215.refs_0_, f32[48,1024]{1,0:T(8,128)S(1)} %get-tuple-element.216.refs_1_, f32[80,1024]{1,0:T(8,128)S(1)} %get-tuple-element.218.refs_3_.refs_2_, ...), custom_call_target="tpu_custom_call" | custom-call | flops 3145728 | bytes 7864320 | tf_op jit(solution)/shard_map/pallas_call | solution.py:394
  51.7 0.0 collective-permute-done.5
  51.8 0.0 collective-permute-done.6
  51.8 0.0 collective-permute-done.7
  51.8 0.6 %fusion.4 = (f32[1,1]{1,0:T(1,128)}, f32[1,1]{1,0:T(1,128)}, f32[1,1]{1,0:T(1,128)}) fusion(f32[1,128]{1,0:T(1,128)S(1)} %add_add_fusion), kind=kLoop, calls=%fused_computation.22 | loop fusion | bytes 24 | tf_op jit(solution)/shard_map/slice | solution.py:418
  52.4 0.0 copy-done.1
  52.4 0.0 copy-done.4
  52.4 0.0 copy-done.6
  52.4 0.0 copy-done.8
  52.4 0.8 %while.42 = (f32[]{:T(128)}, f32[]{:T(128)}, f32[48,8,1024]{2,1,0:T(8,128)}, f32[]{:T(128)}, s32[48,8,1024]{2,1,0:T(8,128)S(1)}, /*index=5*/s32[8,1024]{1,0:T(8,...) while((f32[]{:T(128)}, f32[]{:T(128)}, ...), condition=%wide.region_10.0_spmd, body=%wide.region_0.10_spmd.sunk | while | flops 17752440 | bytes 52235400 | solution.py:419
  (1 shorter events, 0.0 us)
Async XLA Ops:
  2.1 14.9 %collective-permute-start.2 = (f32[200,1024]{1,0:T(8,128)S(1)}, f32[200,1024]{1,0:T(8,128)S(1)}, u32[]{:S(2)}, u32[]{:S(2)}) collective-permute-start(f32[200,1024]{1,0:T(8,128)S(1)} %get-tuple-element.215.refs_0_), channel_id=1, source_target_pairs={{1,0},{2,1},{3,2},{4,3},{5,4},{6,5},{7,6},{8,7},{9,8},{10,9},{11,1... | collective-permute-start | bytes 2457608 | tf_op jit(solution)/shard_map/ppermute | solution.py:349
  7.3 5.9 %collective-permute-start.4 = (f32[80,1024]{1,0:T(8,128)S(1)}, f32[80,1024]{1,0:T(8,128)S(1)}, u32[]{:S(2)}, u32[]{:S(2)}) collective-permute-start(f32[80,1024]{1,0:T(8,128)S(1)} %get-tuple-element.218.refs_3_.refs_2_), channel_id=1, source_target_pairs={{0,1},{1,2},{2,3},{3,4},{4,5},{5,6},{6,7},{7,8},{8,9},{9,10},{10,1... | collective-permute-start | bytes 983048 | tf_op jit(solution)/shard_map/ppermute | solution.py:352
  9.2 10.3 %collective-permute-start.3 = (f32[72,1024]{1,0:T(8,128)S(1)}, f32[72,1024]{1,0:T(8,128)S(1)}, u32[]{:S(2)}, u32[]{:S(2)}) collective-permute-start(f32[72,1024]{1,0:T(8,128)S(1)} %get-tuple-element.217.refs_3_), channel_id=1, source_target_pairs={{0,1},{1,2},{2,3},{3,4},{4,5},{5,6},{6,7},{7,8},{8,9},{9,10},{10,1... | collective-permute-start | bytes 884744 | tf_op jit(solution)/shard_map/ppermute | solution.py:352
  44.6 7.1 %collective-permute-start.5 = (f32[1,128]{1,0:T(1,128)S(1)}, f32[1,128]{1,0:T(1,128)S(1)}, u32[]{:S(2)}, u32[]{:S(2)}) collective-permute-start(f32[1,128]{1,0:T(1,128)S(1)} %get-tuple-element.221), channel_id=1, source_target_pairs={{0,128},{64,192},{128,0},{192,64},{1,129},{65,193},{129,1},{193,65... | collective-permute-start | bytes 1544 | tf_op jit(solution)/shard_map/ppermute | solution.py:387
  47.6 4.1 %collective-permute-start.6 = (f32[1,128]{1,0:T(1,128)S(1)}, f32[1,128]{1,0:T(1,128)S(1)}, u32[]{:S(2)}, u32[]{:S(2)}) collective-permute-start(f32[1,128]{1,0:T(1,128)S(1)} %get-tuple-element.221), channel_id=1, source_target_pairs={{0,64},{64,128},{128,192},{192,0},{1,65},{65,129},{129,193},{193,1... | collective-permute-start | bytes 1544 | tf_op jit(solution)/shard_map/ppermute | solution.py:387
  48.0 3.8 %collective-permute-start.7 = (f32[1,128]{1,0:T(1,128)S(1)}, f32[1,128]{1,0:T(1,128)S(1)}, u32[]{:S(2)}, u32[]{:S(2)}) collective-permute-start(f32[1,128]{1,0:T(1,128)S(1)} %get-tuple-element.221), channel_id=1, source_target_pairs={{0,192},{64,0},{128,64},{192,128},{1,193},{65,1},{129,65},{193,129... | collective-permute-start | bytes 1544 | tf_op jit(solution)/shard_map/ppermute | solution.py:387
  50.3 2.1 %copy-start.1 = (s32[48,8,1024]{2,1,0:T(8,128)S(1)}, s32[48,8,1024]{2,1,0:T(8,128)}, u32[]{:S(2)}) copy-start(s32[48,8,1024]{2,1,0:T(8,128)} %signs_hbm.1) | copy-start | bytes 4718596
  50.3 2.1 %copy-start.4 = (s32[8,1024]{1,0:T(8,128)S(1)}, s32[8,1024]{1,0:T(8,128)}, u32[]{:S(2)}) copy-start(s32[8,1024]{1,0:T(8,128)} %mask_hbm.1) | copy-start | bytes 98308
  50.3 2.1 %copy-start.6 = (f32[8,1024]{1,0:T(8,128)S(1)}, f32[8,1024]{1,0:T(8,128)}, u32[]{:S(2)}) copy-start(f32[8,1024]{1,0:T(8,128)} %weight_hbm.1) | copy-start | bytes 98308
  50.3 2.1 %copy-start.8 = (f32[8,1024]{1,0:T(8,128)S(1)}, f32[8,1024]{1,0:T(8,128)}, u32[]{:S(2)}) copy-start(f32[8,1024]{1,0:T(8,128)} %mass_hbm.1) | copy-start | bytes 98308

commit v3 on v2

--- a/solution.py
+++ b/solution.py
@@ -61,13 +61,22 @@
     return solution, trace_sum / float(probes.shape[0] * lax.axis_size("probe") * cells)
 
 
+def reach(n):
+    return (3, 4) if n % 2 == 0 else (4, 3)
+
+
+def up_start(n, count):
+    return sum(reach(m)[1] for m in range(n)) * count
+
+
 def edge_of(r, n, count, refs):
     up_ref, mid_ref, *dn_refs = refs
-    if r < 4:
-        return up_ref, (r * CHUNKS + n) * count
-    if r == 4:
+    _, below = reach(n)
+    if r < below:
+        return up_ref, up_start(n, count) + r * count
+    if r == below:
         return mid_ref, n * count
-    return dn_refs[n], (r - 5) * count
+    return dn_refs[n], (r - below - 1) * count
 
 
 def prepare_kernel(signs_hbm, mask_hbm, weight_hbm, mass_hbm, *refs):
@@ -98,8 +107,8 @@
     for copy in copies[groups:]:
         copy.wait()
     diagonal = mask_ref[...].astype(jnp.float32) * weight_ref[...] + mass_ref[...]
-    outs[0][4 * probes :, :] = diagonal
-    outs[2][3 * count :, :] = diagonal
+    outs[0][up_start(CHUNKS, count) :, :] = diagonal
+    outs[2][reach(0)[0] * count :, :] = diagonal
 
 
 def powers_kernel(chunk, *refs):
@@ -112,6 +121,7 @@
         v1_ref, v2_ref, v3_ref, part_ref, dd_ref, h1_ref, h2_ref, h3_ref = refs[5:]
     rows, probes, columns = v1_ref.shape
     tiles = columns // LANES
+    edges = [up_ref, mid_ref] + [dn_ref] * CHUNKS
     lane = lax.broadcasted_iota(jnp.int32, (GROUP, LANES), 1)
     first, last = lane == 0, lane == LANES - 1
     nothing = jnp.zeros((GROUP, LANES), jnp.float32)
@@ -124,18 +134,22 @@
         dd_ref[to] = jnp.broadcast_to(line + (4.0 - SHIFT), (GROUP, columns))
         return jnp.where(jnp.broadcast_to(line[:, :LANES], (GROUP, LANES)) > 0.0, 1.0, 0.0)
 
-    spread(above_dd_ref, 3 * probes + 6, 0)
-    in_above = spread(above_dd_ref, 3 * probes + 7, 1)
+    above_rows, below_rows = reach(chunk)
+    low = 1 - above_rows
+    for r in range(low, 0):
+        in_above = spread(above_dd_ref, reach(0)[0] * probes + rows + r, r - low)
     for r in range(rows):
-        spread(up_ref, 4 * CHUNKS * probes + r, r + 2)
-    in_below = spread(below_ref, 4 * CHUNKS * probes, 10)
-    spread(below_ref, 4 * CHUNKS * probes + 1, 11)
-    spread(below_ref, 4 * CHUNKS * probes + 2, 12)
+        spread(up_ref, up_start(CHUNKS, probes) + r, r - low)
+    for r in range(rows, rows + below_rows - 1):
+        in_below = spread(below_ref, up_start(CHUNKS, probes) + r - rows, r - low)
     part_ref[7 * probes :, :] = jnp.zeros((probes, LANES), jnp.float32)
 
     own = [None, v1_ref, v2_ref, v3_ref]
     halo = [None, h1_ref, h2_ref, h3_ref]
-    place = [None, {-2: 0, -1: 1, 8: 2, 9: 3, 10: 4}, {-1: 0, 8: 1, 9: 2}, {8: 0}]
+    spans = [(k + 1 - above_rows, rows + below_rows - 1 - k) for k in range(3)]
+    place = [None]
+    for begin, end in spans:
+        place.append({r: n for n, r in enumerate([*range(begin, 0), *range(rows, end)])})
 
     def where(level, r, base):
         if level:
@@ -143,14 +157,11 @@
                 return own[level], (r, pl.ds(base, GROUP))
             return halo[level], (place[level][r], slice(None))
         if r < 0:
-            return above_ref, (pl.ds((r + 3) * probes + base, GROUP),)
-        if r < 4:
-            return up_ref, (pl.ds((r * CHUNKS + chunk) * probes + base, GROUP),)
-        if r == 4:
-            return mid_ref, (pl.ds(chunk * probes + base, GROUP),)
-        if r < rows:
-            return dn_ref, (pl.ds((r - 5) * probes + base, GROUP),)
-        return below_ref, (pl.ds(((r - rows) * CHUNKS + chunk) * probes + base, GROUP),)
+            return above_ref, (pl.ds((r + above_rows) * probes + base, GROUP),)
+        if r >= rows:
+            return below_ref, (pl.ds(up_start(chunk, probes) + (r - rows) * probes + base, GROUP),)
+        ref, start = edge_of(r, chunk, probes, edges)
+        return ref, (pl.ds(start + base, GROUP),)
 
     def sideways(v):
         left = [pltpu.roll(t, 1, 1) for t in v]
@@ -170,7 +181,7 @@
             return [ref[index + (at(c),)] for c in range(tiles)]
 
         totals = []
-        for level, (begin, end) in enumerate([(-2, 11), (-1, 10), (0, 9)]):
+        for level, (begin, end) in enumerate(spans):
             cross, square = nothing, nothing
             before, here = line(level, begin - 1), line(level, begin)
             for r in range(begin, end):
@@ -178,7 +189,7 @@
                 side = sideways(here)
                 ref, index = where(level + 1, r, base)
                 for c in range(tiles):
-                    value = dd_ref[r + 2, :, at(c)] * here[c] - (side[c] + (before[c] + after[c]))
+                    value = dd_ref[r - low, :, at(c)] * here[c] - (side[c] + (before[c] + after[c]))
                     if r < 0:
                         value = in_above * value
                     if r >= rows:
@@ -190,13 +201,17 @@
                 before, here = here, after
             totals += [cross, square]
         quad = nothing
-        here = line(3, 0)
+        if below_rows < above_rows:
+            beyond = line(3, -1)
         for r in range(rows):
-            after = line(3, r + 1)
-            side = sideways(here)
+            here = line(3, r)
+            if below_rows > above_rows:
+                beyond = line(3, r + 1)
+            right = [pltpu.roll(t, LANES - 1, 1) for t in here]
             for c in range(tiles):
-                quad = quad + here[c] * (dd_ref[r + 2, :, at(c)] * here[c] - (side[c] + (after[c] + after[c])))
-            here = after
+                beside = jnp.where(last, right[c + 1] if c + 1 < tiles else nothing, right[c]) + beyond[c]
+                quad = quad + here[c] * (dd_ref[r - low, :, at(c)] * here[c] - (beside + beside))
+            beyond = here
         totals.append(quad)
         for k, total in enumerate(totals):
             part_ref[pl.ds(k * probes + base, GROUP), :] = total
@@ -334,8 +349,8 @@
         prepare_kernel,
         in_specs=[HBM] * 4,
         out_specs=[VMEM] * (CHUNKS + 2),
-        out_shape=[shaped(4 * probes + rows, columns), shaped(probes, columns)]
-        + [shaped(3 * count + (0 if n else rows), columns) for n in range(CHUNKS)],
+        out_shape=[shaped(up_start(CHUNKS, count) + rows, columns), shaped(probes, columns)]
+        + [shaped(reach(n)[0] * count + (0 if n else rows), columns) for n in range(CHUNKS)],
         scratch_shapes=[
             pltpu.VMEM((probes, rows, columns), jnp.int32),
             pltpu.VMEM((rows, columns), jnp.int32),

time: 53.7 us -> 55.3 us (1.030)
  blocking collectives: 21.9 us -> 23.4 us
    ppermute x2, waiting for transfers between devices: 1.77 us -> 5.98 us  [on_device(): lax.ppermute(dn, 'space', [(i, i + 1) for i in range(strips - 1)])]
    ppermute x1, waiting for transfers between devices: 3.9 us -> 0.01 us  [on_device(): below = lax.ppermute(up, 'space', [(i + 1, i) for i in range(strips - 1)])]
    all_to_all x1, blocking collectives: 21.9 us -> 23.4 us  [on_device(): lax.all_to_all(powers[-1][3], 'space', split_axis=0, concat_axis=0, tiled...]
  transfers between devices with their start and end apart: 6 -> 6, of which waited for: 2 -> 1; matrix products, arithmetic and copies ran while one was open for 0% -> 0% of each run, Pallas kernels for 7% -> 7%
where the time goes in v3:
time: 55.3 us; the launch traced here: 55.1 us
  blocking collectives  23.4 us (42%)
  starting transfers between devices  14.9 us (27%)
  Pallas kernels  8.38 us (15%)
  waiting for transfers between devices  5.99 us (11%)
  between operations  0.9 us (2%)
  loops' own time  0.82 us (1%)
  local copies, waits for them, and re-layouts  0.63 us (1%)
    all_to_all x1, blocking collectives, on_device(): lax.all_to_all(powers[-1][3], 'space', split_axis=0, concat_axis=0, tiled...  23.4 us
    ppermute x2, waiting for transfers between devices, on_device(): lax.ppermute(dn, 'space', [(i, i + 1) for i in range(strips - 1)])  5.98 us
    ppermute x3, starting transfers between devices, on_device(): lax.ppermute(trace, 'probe', [(i, (i + k) % groups) for i in range(groups)])  5.67 us
    ppermute x1, starting transfers between devices, on_device(): below = lax.ppermute(up, 'space', [(i + 1, i) for i in range(strips - 1)])  5.11 us
    pallas_call x2, Pallas kernels, on_device(): pl.pallas_call(functools.partial(powers_kernel, n), in_specs=[VMEM] * len...  5.01 us
    ppermute x2, starting transfers between devices, on_device(): lax.ppermute(dn, 'space', [(i, i + 1) for i in range(strips - 1)])  4.14 us
    pallas_call x1, Pallas kernels, on_device(): pl.pallas_call(prepare_kernel, in_specs=[HBM] * 4, out_specs=[VMEM] * (CH...  1.51 us
    pallas_call x1, Pallas kernels, on_device(): pl.pallas_call(combine_kernel, in_specs=[VMEM] * len(args), out_specs=HBM...  1.43 us
  transfers between devices with their start and end apart: 6, of which 1 were waited for; matrix products, arithmetic and copies ran while one was open for 0% of the time, Pallas kernels for 7%

profile of v3, /device:TPU:1, one launch (start us, length us, event | category | flops | bytes accessed | tf_op | source)
XLA Modules:
  0.0 55.1 jit_solution(9917149046210160293)
XLA Ops:
  0.6 1.5 %shard_map.59 = (f32[176,1024]{1,0:T(8,128)S(1)}, f32[48,1024]{1,0:T(8,128)S(1)}, f32[80,1024]{1,0:T(8,128)S(1)}, f32[96,1024]{1,0:T(8,128)S(1)}) custom-call(s32[48,8,1024]{2,1,0:T(8,128)} %signs_hbm.1, s32[8,1024]{1,0:T(8,128)} %mask_hbm.1, f32[8,1024]{1,0:T(8,128)} %weight_hbm.1, f32[8,1024]{1,0:T(8,128)} %mass_hbm.1), custom_call_target="tpu_custom_call" | custom-call | tf_op jit(solution)/shard_map/pallas_call | solution.py:348
  2.1 5.1 %collective-permute-start.2 = (f32[176,1024]{1,0:T(8,128)S(1)}, f32[176,1024]{1,0:T(8,128)S(1)}, u32[]{:S(2)}, u32[]{:S(2)}) collective-permute-start(f32[176,1024]{1,0:T(8,128)S(1)} %get-tuple-element.215.refs_0_), channel_id=1, source_target_pairs={{1,0},{2,1},{3,2},{4,3},{5,4},{6,5},{7,6},{8,7},{9,8},{10,9},{11,1... | collective-permute-start | bytes 2162696 | tf_op jit(solution)/shard_map/ppermute | solution.py:364
  7.3 1.9 %collective-permute-start.3 = (f32[96,1024]{1,0:T(8,128)S(1)}, f32[96,1024]{1,0:T(8,128)S(1)}, u32[]{:S(2)}, u32[]{:S(2)}) collective-permute-start(f32[96,1024]{1,0:T(8,128)S(1)} %get-tuple-element.217.refs_3_), channel_id=1, source_target_pairs={{0,1},{1,2},{2,3},{3,4},{4,5},{5,6},{6,7},{7,8},{8,9},{9,10},{10,1... | collective-permute-start | bytes 1179656 | tf_op jit(solution)/shard_map/ppermute | solution.py:367
  9.2 2.2 %collective-permute-start.4 = (f32[80,1024]{1,0:T(8,128)S(1)}, f32[80,1024]{1,0:T(8,128)S(1)}, u32[]{:S(2)}, u32[]{:S(2)}) collective-permute-start(f32[80,1024]{1,0:T(8,128)S(1)} %get-tuple-element.218.refs_3_.refs_2_), channel_id=1, source_target_pairs={{0,1},{1,2},{2,3},{3,4},{4,5},{5,6},{6,7},{7,8},{8,9},{9,10},{10,1... | collective-permute-start | bytes 983048 | tf_op jit(solution)/shard_map/ppermute | solution.py:367
  11.4 6.0 %collective-permute-done.4.refs_4_.refs_5_ = f32[80,1024]{1,0:T(8,128)S(1)} collective-permute-done((f32[80,1024]{1,0:T(8,128)S(1)}, f32[80,1024]{1,0:T(8,128)S(1)}, u32[]{:S(2)}, u32[]{:S(2)}) %collective-permute-start.4) | collective-permute-done | bytes 327712 | tf_op jit(solution)/shard_map/ppermute | solution.py:367
  17.4 0.0 collective-permute-done.2.refs_2_
  17.4 2.2 %shard_map.60 = (f32[8,24,1024]{2,1,0:T(8,128)S(1)}, f32[8,24,1024]{2,1,0:T(8,128)S(1)}, f32[8,24,1024]{2,1,0:T(8,128)S(1)}, f32[192,128]{1,0:T(8,128)S(1)}) custom-call(f32[176,1024]{1,0:T(8,128)S(1)} %get-tuple-element.215.refs_0_, f32[48,1024]{1,0:T(8,128)S(1)} %get-tuple-element.216.refs_1_, f32[176,1024]{1,0:T(8,128)S(1)} %collective-permute-done.2.refs_2_, ...), custom_call_target="tpu_custom_call" | custom-call | tf_op jit(solution)/shard_map/pallas_call | solution.py:380
  19.7 0.0 collective-permute-done.3.refs_4_
  19.7 2.8 %shard_map.61 = (f32[8,24,1024]{2,1,0:T(8,128)S(1)}, f32[8,24,1024]{2,1,0:T(8,128)S(1)}, f32[8,24,1024]{2,1,0:T(8,128)S(1)}, f32[64,1,384]{2,1,0:T(1,128)S(1)}) custom-call(f32[176,1024]{1,0:T(8,128)S(1)} %get-tuple-element.215.refs_0_, f32[48,1024]{1,0:T(8,128)S(1)} %get-tuple-element.216.refs_1_, f32[176,1024]{1,0:T(8,128)S(1)} %collective-permute-done.2.refs_2_, ...), custom_call_target="tpu_custom_call" | custom-call | tf_op jit(solution)/shard_map/pallas_call | solution.py:380
  22.4 23.4 %all_to_all.49.sums_ref = f32[64,1,384]{2,1,0:T(1,128)S(1)} all-to-all(f32[64,1,384]{2,1,0:T(1,128)S(1)} %get-tuple-element.220), channel_id=1, replica_groups=mesh['probe'=4,'space'=64] {'space'}, dimensions={0} | all-to-all | bytes 196608 | tf_op jit(solution)/shard_map/all_to_all | solution.py:390
  45.9 0.4 shard_map.62
  46.3 3.0 %collective-permute-start.5 = (f32[1,128]{1,0:T(1,128)S(1)}, f32[1,128]{1,0:T(1,128)S(1)}, u32[]{:S(2)}, u32[]{:S(2)}) collective-permute-start(f32[1,128]{1,0:T(1,128)S(1)} %get-tuple-element.221), channel_id=1, source_target_pairs={{0,128},{64,192},{128,0},{192,64},{1,129},{65,193},{129,1},{193,65... | collective-permute-start | bytes 1544 | tf_op jit(solution)/shard_map/ppermute | solution.py:402
  49.3 0.4 collective-permute-start.6
  49.7 2.3 %collective-permute-start.7 = (f32[1,128]{1,0:T(1,128)S(1)}, f32[1,128]{1,0:T(1,128)S(1)}, u32[]{:S(2)}, u32[]{:S(2)}) collective-permute-start(f32[1,128]{1,0:T(1,128)S(1)} %get-tuple-element.221), channel_id=1, source_target_pairs={{0,192},{64,0},{128,64},{192,128},{1,193},{65,1},{129,65},{193,129... | collective-permute-start | bytes 1544 | tf_op jit(solution)/shard_map/ppermute | solution.py:402
  52.0 0.0 copy-start.1
  52.0 0.0 copy-start.4
  52.0 0.0 copy-start.6
  52.0 0.0 copy-start.8
  52.0 1.4 %shard_map.63 = f32[48,8,1024]{2,1,0:T(8,128)} custom-call(f32[192,128]{1,0:T(8,128)S(1)} %get-tuple-element.222.coef_ref, f32[176,1024]{1,0:T(8,128)S(1)} %get-tuple-element.215.refs_0_, f32[48,1024]{1,0:T(8,128)S(1)} %get-tuple-element.216.refs_1_, f32[80,1024]{1,0:T(8,128)S(1)} %get-tuple-element.218.refs_3_.refs_2_, ...), custom_call_target="tpu_custom_call" | custom-call | flops 3145728 | bytes 7864320 | tf_op jit(solution)/shard_map/pallas_call | solution.py:409
  53.4 0.0 collective-permute-done.5
  53.4 0.0 collective-permute-done.6
  53.4 0.0 collective-permute-done.7
  53.5 0.6 %fusion.4 = (f32[1,1]{1,0:T(1,128)}, f32[1,1]{1,0:T(1,128)}, f32[1,1]{1,0:T(1,128)}) fusion(f32[1,128]{1,0:T(1,128)S(1)} %add_add_fusion), kind=kLoop, calls=%fused_computation.22 | loop fusion | bytes 24 | tf_op jit(solution)/shard_map/slice | solution.py:433
  54.1 0.0 copy-done.1
  54.1 0.0 copy-done.4
  54.1 0.0 copy-done.6
  54.1 0.0 copy-done.8
  54.1 0.8 %while.42 = (f32[]{:T(128)}, f32[]{:T(128)}, f32[48,8,1024]{2,1,0:T(8,128)}, f32[]{:T(128)}, s32[48,8,1024]{2,1,0:T(8,128)S(1)}, /*index=5*/s32[8,1024]{1,0:T(8,...) while((f32[]{:T(128)}, f32[]{:T(128)}, ...), condition=%wide.region_10.0_spmd, body=%wide.region_0.10_spmd.sunk | while | flops 17752440 | bytes 52235400 | solution.py:434
  (1 shorter events, 0.0 us)
Async XLA Ops:
  2.1 15.3 %collective-permute-start.2 = (f32[176,1024]{1,0:T(8,128)S(1)}, f32[176,1024]{1,0:T(8,128)S(1)}, u32[]{:S(2)}, u32[]{:S(2)}) collective-permute-start(f32[176,1024]{1,0:T(8,128)S(1)} %get-tuple-element.215.refs_0_), channel_id=1, source_target_pairs={{1,0},{2,1},{3,2},{4,3},{5,4},{6,5},{7,6},{8,7},{9,8},{10,9},{11,1... | collective-permute-start | bytes 2162696 | tf_op jit(solution)/shard_map/ppermute | solution.py:364
  7.3 12.4 %collective-permute-start.3 = (f32[96,1024]{1,0:T(8,128)S(1)}, f32[96,1024]{1,0:T(8,128)S(1)}, u32[]{:S(2)}, u32[]{:S(2)}) collective-permute-start(f32[96,1024]{1,0:T(8,128)S(1)} %get-tuple-element.217.refs_3_), channel_id=1, source_target_pairs={{0,1},{1,2},{2,3},{3,4},{4,5},{5,6},{6,7},{7,8},{8,9},{9,10},{10,1... | collective-permute-start | bytes 1179656 | tf_op jit(solution)/shard_map/ppermute | solution.py:367
  9.2 8.2 %collective-permute-start.4 = (f32[80,1024]{1,0:T(8,128)S(1)}, f32[80,1024]{1,0:T(8,128)S(1)}, u32[]{:S(2)}, u32[]{:S(2)}) collective-permute-start(f32[80,1024]{1,0:T(8,128)S(1)} %get-tuple-element.218.refs_3_.refs_2_), channel_id=1, source_target_pairs={{0,1},{1,2},{2,3},{3,4},{4,5},{5,6},{6,7},{7,8},{8,9},{9,10},{10,1... | collective-permute-start | bytes 983048 | tf_op jit(solution)/shard_map/ppermute | solution.py:367
  46.3 7.1 %collective-permute-start.5 = (f32[1,128]{1,0:T(1,128)S(1)}, f32[1,128]{1,0:T(1,128)S(1)}, u32[]{:S(2)}, u32[]{:S(2)}) collective-permute-start(f32[1,128]{1,0:T(1,128)S(1)} %get-tuple-element.221), channel_id=1, source_target_pairs={{0,128},{64,192},{128,0},{192,64},{1,129},{65,193},{129,1},{193,65... | collective-permute-start | bytes 1544 | tf_op jit(solution)/shard_map/ppermute | solution.py:402
  49.3 4.1 %collective-permute-start.6 = (f32[1,128]{1,0:T(1,128)S(1)}, f32[1,128]{1,0:T(1,128)S(1)}, u32[]{:S(2)}, u32[]{:S(2)}) collective-permute-start(f32[1,128]{1,0:T(1,128)S(1)} %get-tuple-element.221), channel_id=1, source_target_pairs={{0,64},{64,128},{128,192},{192,0},{1,65},{65,129},{129,193},{193,1... | collective-permute-start | bytes 1544 | tf_op jit(solution)/shard_map/ppermute | solution.py:402
  49.7 3.8 %collective-permute-start.7 = (f32[1,128]{1,0:T(1,128)S(1)}, f32[1,128]{1,0:T(1,128)S(1)}, u32[]{:S(2)}, u32[]{:S(2)}) collective-permute-start(f32[1,128]{1,0:T(1,128)S(1)} %get-tuple-element.221), channel_id=1, source_target_pairs={{0,192},{64,0},{128,64},{192,128},{1,193},{65,1},{129,65},{193,129... | collective-permute-start | bytes 1544 | tf_op jit(solution)/shard_map/ppermute | solution.py:402
  52.0 2.1 %copy-start.1 = (s32[48,8,1024]{2,1,0:T(8,128)S(1)}, s32[48,8,1024]{2,1,0:T(8,128)}, u32[]{:S(2)}) copy-start(s32[48,8,1024]{2,1,0:T(8,128)} %signs_hbm.1) | copy-start | bytes 4718596
  52.0 2.1 %copy-start.4 = (s32[8,1024]{1,0:T(8,128)S(1)}, s32[8,1024]{1,0:T(8,128)}, u32[]{:S(2)}) copy-start(s32[8,1024]{1,0:T(8,128)} %mask_hbm.1) | copy-start | bytes 98308
  52.0 2.1 %copy-start.6 = (f32[8,1024]{1,0:T(8,128)S(1)}, f32[8,1024]{1,0:T(8,128)}, u32[]{:S(2)}) copy-start(f32[8,1024]{1,0:T(8,128)} %weight_hbm.1) | copy-start | bytes 98308
  52.0 2.1 %copy-start.8 = (f32[8,1024]{1,0:T(8,128)S(1)}, f32[8,1024]{1,0:T(8,128)}, u32[]{:S(2)}) copy-start(f32[8,1024]{1,0:T(8,128)} %mass_hbm.1) | copy-start | bytes 98308

commit v4 on v3

--- a/solution.py
+++ b/solution.py
@@ -13,6 +13,7 @@
 LANES = 128
 GROUP = 8
 CHUNKS = 2
+ROWS = 8
 AMPLIFIED = 600.0
 VMEM_LIMIT = 16 * 1024 * 1024
 
@@ -111,55 +112,78 @@
     outs[2][reach(0)[0] * count :, :] = diagonal
 
 
-def powers_kernel(chunk, *refs):
-    up_ref, mid_ref, below_ref, dn_ref, above_ref = refs[:5]
-    if chunk:
-        above_dd_ref, earlier_ref = refs[5:7]
-        v1_ref, v2_ref, v3_ref, sums_ref, dd_ref, h1_ref, h2_ref, h3_ref, total_ref, part_ref = refs[7:]
+def owner(level, r, rows):
+    return 0 if level <= r < rows - level else 1 if r >= rows - level else 2
+
+
+def kept(stage, level, rows):
+    return [(level, rows - 2 * level), (rows - level, level), (0, level)][stage]
+
+
+def powers_kernel(stage, chunk, final, *refs):
+    refs = list(refs)
+    edges = [refs.pop(0), refs.pop(0)]
+    dn_ref = refs.pop(0)
+    edges += [dn_ref] * CHUNKS
+    up_ref = edges[0]
+    side_ref = refs.pop(0) if stage else None
+    far_ref = refs.pop(0) if stage else None
+    middle = [None] + [refs.pop(0) for _ in range(ITERS - 1)] if stage else None
+    before_ref = refs.pop(0) if stage else None
+    earlier_ref = refs.pop(0) if final else None
+    own = [None] + [refs.pop(0) for _ in range(ITERS - 1)]
+    if final:
+        sums_ref, dd_ref, h1_ref, h2_ref, h3_ref, total_ref, part_ref = refs
     else:
-        above_dd_ref = above_ref
-        v1_ref, v2_ref, v3_ref, part_ref, dd_ref, h1_ref, h2_ref, h3_ref = refs[5:]
-    rows, probes, columns = v1_ref.shape
+        part_ref, dd_ref, h1_ref, h2_ref, h3_ref = refs
+    halo = [None, h1_ref, h2_ref, h3_ref]
+    _, probes, columns = own[1].shape
+    rows = ROWS
     tiles = columns // LANES
-    edges = [up_ref, mid_ref] + [dn_ref] * CHUNKS
     lane = lax.broadcasted_iota(jnp.int32, (GROUP, LANES), 1)
     first, last = lane == 0, lane == LANES - 1
     nothing = jnp.zeros((GROUP, LANES), jnp.float32)
+    above_rows, below_rows = reach(chunk)
 
     def at(c):
         return pl.ds(c * LANES, LANES)
 
-    def spread(ref, row, to):
+    spans = []
+    for level in range(1, ITERS):
+        begin, end = level - above_rows, rows + below_rows - level
+        spans.append([r for r in range(begin, end) if owner(level, r, rows) == stage])
+    upward = below_rows > above_rows
+    corner = [3] if upward else [4]
+    quads = [corner, range(corner[0] + 1, rows), range(corner[0])][stage]
+    low = min(min(spans[0]), min(quads))
+    high = max(max(spans[0]), max(quads))
+
+    inside = None
+    for r in range(low, high + 1):
+        if r < 0:
+            ref, row = far_ref, reach(0)[0] * probes + rows + r
+        elif r < rows:
+            ref, row = up_ref, up_start(CHUNKS, probes) + r
+        else:
+            ref, row = far_ref, up_start(CHUNKS, probes) + r - rows
         line = ref[row : row + 1, :]
-        dd_ref[to] = jnp.broadcast_to(line + (4.0 - SHIFT), (GROUP, columns))
-        return jnp.where(jnp.broadcast_to(line[:, :LANES], (GROUP, LANES)) > 0.0, 1.0, 0.0)
-
-    above_rows, below_rows = reach(chunk)
-    low = 1 - above_rows
-    for r in range(low, 0):
-        in_above = spread(above_dd_ref, reach(0)[0] * probes + rows + r, r - low)
-    for r in range(rows):
-        spread(up_ref, up_start(CHUNKS, probes) + r, r - low)
-    for r in range(rows, rows + below_rows - 1):
-        in_below = spread(below_ref, up_start(CHUNKS, probes) + r - rows, r - low)
-    part_ref[7 * probes :, :] = jnp.zeros((probes, LANES), jnp.float32)
-
-    own = [None, v1_ref, v2_ref, v3_ref]
-    halo = [None, h1_ref, h2_ref, h3_ref]
-    spans = [(k + 1 - above_rows, rows + below_rows - 1 - k) for k in range(3)]
-    place = [None]
-    for begin, end in spans:
-        place.append({r: n for n, r in enumerate([*range(begin, 0), *range(rows, end)])})
+        dd_ref[r - low] = jnp.broadcast_to(line + (4.0 - SHIFT), (GROUP, columns))
+        if not 0 <= r < rows:
+            inside = jnp.where(jnp.broadcast_to(line[:, :LANES], (GROUP, LANES)) > 0.0, 1.0, 0.0)
 
     def where(level, r, base):
+        mine = pl.ds(base, GROUP)
         if level:
-            if 0 <= r < rows:
-                return own[level], (r, pl.ds(base, GROUP))
-            return halo[level], (place[level][r], slice(None))
+            if not 0 <= r < rows:
+                n = r - rows if r >= rows else r + above_rows - level
+                return halo[level], (n, slice(None))
+            by = owner(level, r, rows)
+            source = own if by == stage else middle
+            return source[level], (r - kept(by, level, rows)[0], mine)
         if r < 0:
-            return above_ref, (pl.ds((r + above_rows) * probes + base, GROUP),)
+            return side_ref, (pl.ds((r + above_rows) * probes + base, GROUP),)
         if r >= rows:
-            return below_ref, (pl.ds(up_start(chunk, probes) + (r - rows) * probes + base, GROUP),)
+            return side_ref, (pl.ds(up_start(chunk, probes) + (r - rows) * probes + base, GROUP),)
         ref, start = edge_of(r, chunk, probes, edges)
         return ref, (pl.ds(start + base, GROUP),)
 
@@ -181,19 +205,17 @@
             return [ref[index + (at(c),)] for c in range(tiles)]
 
         totals = []
-        for level, (begin, end) in enumerate(spans):
+        for level, span in enumerate(spans):
             cross, square = nothing, nothing
-            before, here = line(level, begin - 1), line(level, begin)
-            for r in range(begin, end):
+            before, here = line(level, span[0] - 1), line(level, span[0])
+            for r in span:
                 after = line(level, r + 1)
                 side = sideways(here)
                 ref, index = where(level + 1, r, base)
                 for c in range(tiles):
                     value = dd_ref[r - low, :, at(c)] * here[c] - (side[c] + (before[c] + after[c]))
-                    if r < 0:
-                        value = in_above * value
-                    if r >= rows:
-                        value = in_below * value
+                    if not 0 <= r < rows:
+                        value = inside * value
                     ref[index + (at(c),)] = value
                     if 0 <= r < rows:
                         cross = cross + here[c] * value
@@ -201,24 +223,22 @@
                 before, here = here, after
             totals += [cross, square]
         quad = nothing
-        if below_rows < above_rows:
-            beyond = line(3, -1)
-        for r in range(rows):
+        for r in quads:
             here = line(3, r)
-            if below_rows > above_rows:
-                beyond = line(3, r + 1)
+            beyond = line(3, r + 1 if upward else r - 1)
             right = [pltpu.roll(t, LANES - 1, 1) for t in here]
             for c in range(tiles):
                 beside = jnp.where(last, right[c + 1] if c + 1 < tiles else nothing, right[c]) + beyond[c]
                 quad = quad + here[c] * (dd_ref[r - low, :, at(c)] * here[c] - (beside + beside))
-            beyond = here
         totals.append(quad)
         for k, total in enumerate(totals):
-            part_ref[pl.ds(k * probes + base, GROUP), :] = total
+            mine = pl.ds(k * probes + base, GROUP)
+            part_ref[mine, :] = total + before_ref[mine, :] if stage else total
         return carry
 
     lax.fori_loop(0, probes // GROUP, group, 0)
-    if not chunk:
+    part_ref[7 * probes :, :] = jnp.zeros((probes, LANES), jnp.float32)
+    if not final:
         return
     for k in range(8):
         begin = k * CHUNKS * probes
@@ -305,8 +325,8 @@
 
 def combine_kernel(coef_ref, *refs):
     edges = refs[: CHUNKS + 2]
-    powers = [refs[CHUNKS + 2 + 3 * n : CHUNKS + 5 + 3 * n] for n in range(CHUNKS)]
-    out_ref, made_ref, sems = refs[4 * CHUNKS + 2 :]
+    powers = [refs[CHUNKS + 2 + 9 * n : CHUNKS + 11 + 9 * n] for n in range(CHUNKS)]
+    out_ref, made_ref, sems = refs[10 * CHUNKS + 2 :]
     probes, rows, columns = made_ref.shape
     count = probes // CHUNKS
 
@@ -317,7 +337,11 @@
     for g in range(probes // GROUP):
         base = g * GROUP
         chunk, local = divmod(base, count)
-        v1_ref, v2_ref, v3_ref = powers[chunk]
+
+        def power(level, r):
+            by = owner(level, r, rows)
+            return powers[chunk][3 * by + level - 1][r - kept(by, level, rows)[0], mine, at]
+
         mine = slice(local, local + GROUP)
         c = [coef_ref[k * probes + base : k * probes + base + GROUP, :] for k in range(ITERS)]
         for t in range(columns // LANES):
@@ -327,7 +351,7 @@
                 ref, start = edge_of(r, chunk, count, edges)
                 probe = ref[start + local : start + local + GROUP, at]
                 made.append(
-                    (c[0] * probe + c[1] * v1_ref[r, mine, at]) + (c[2] * v2_ref[r, mine, at] + c[3] * v3_ref[r, mine, at])
+                    (c[0] * probe + c[1] * power(1, r)) + (c[2] * power(2, r) + c[3] * power(3, r))
                 )
             made_ref[base : base + GROUP, :, at] = jnp.swapaxes(jnp.stack(made), 0, 1)
         copy(g).start()
@@ -366,28 +390,33 @@
     for dn in downs:
         above.append(lax.ppermute(dn, "space", [(i, i + 1) for i in range(strips - 1)]))
 
-    field = shaped(rows, count, columns)
-    powers = []
-    for n in range(CHUNKS):
-        args = [up, mid, below, downs[n], above[n]]
-        sums = shaped(8 * count, LANES)
-        scratch = [pltpu.VMEM((size, GROUP, columns), jnp.float32) for size in (rows + 5, 5, 3, 1)]
-        if n:
-            args += [above[0], powers[0][3]]
-            sums = shaped(strips, 1, 8 * probes)
-            scratch += [pltpu.VMEM((8 * probes, LANES), jnp.float32), pltpu.VMEM((8 * count, LANES), jnp.float32)]
-        powers.append(
-            pl.pallas_call(
-                functools.partial(powers_kernel, n),
+    made = [[], []]
+    parts = [None, None]
+    for stage in range(3):
+        for n in range(CHUNKS):
+            final = stage == 2 and n == CHUNKS - 1
+            args = [up, mid, downs[n]]
+            if stage:
+                args += [below, below] if stage == 1 else [above[n], above[0]]
+                args += [*made[n][:3], parts[n]]
+            if final:
+                args.append(parts[0])
+            outs = [shaped(kept(stage, level, rows)[1], count, columns) for level in range(1, ITERS)]
+            outs.append(shaped(strips, 1, 8 * probes) if final else shaped(8 * count, LANES))
+            scratch = [pltpu.VMEM((size, GROUP, columns), jnp.float32) for size in (rows + 5, 3, 2, 1)]
+            if final:
+                scratch += [pltpu.VMEM((8 * probes, LANES), jnp.float32), pltpu.VMEM((8 * count, LANES), jnp.float32)]
+            *fresh, parts[n] = pl.pallas_call(
+                functools.partial(powers_kernel, stage, n, final),
                 in_specs=[VMEM] * len(args),
-                out_specs=[VMEM] * 4,
-                out_shape=[field, field, field, sums],
+                out_specs=[VMEM] * len(outs),
+                out_shape=outs,
                 scratch_shapes=scratch,
                 compiler_params=params,
             )(*args)
-        )
-
-    sums = lax.all_to_all(powers[-1][3], "space", split_axis=0, concat_axis=0, tiled=True)
+            made[n] += fresh
+
+    sums = lax.all_to_all(parts[-1], "space", split_axis=0, concat_axis=0, tiled=True)
 
     cells = float(rows * strips * columns)
     coef, trace = pl.pallas_call(
@@ -404,8 +433,8 @@
     ]
 
     args = [coef, *edges]
-    for power in powers:
-        args += power[:3]
+    for fresh in made:
+        args += fresh
     combined = pl.pallas_call(
         combine_kernel,
         in_specs=[VMEM] * len(args),

time: 55.3 us -> 54.1 us (0.978)
  waiting for transfers between devices: 5.99 us -> 2.78 us
  Pallas kernels: 8.38 us -> 10.2 us
    ppermute x2, waiting for transfers between devices: 5.98 us -> 0.32 us  [on_device(): lax.ppermute(dn, 'space', [(i, i + 1) for i in range(strips - 1)])]
    ppermute x1, waiting for transfers between devices: 0.01 us -> 2.44 us  [on_device(): below = lax.ppermute(up, 'space', [(i + 1, i) for i in range(strips - 1)])]
    pallas_call x2 -> x6, Pallas kernels: 5.01 us -> 6.82 us  [on_device(): pl.pallas_call(functools.partial(powers_kernel, stage, n, final), in_spec...]
  transfers between devices with their start and end apart: 6 -> 6, of which waited for: 1 -> 2; matrix products, arithmetic and copies ran while one was open for 0% -> 0% of each run, Pallas kernels for 7% -> 12%
where the time goes in v4:
time: 54.1 us; the launch traced here: 53.8 us
  blocking collectives  23.4 us (43%)
  starting transfers between devices  14.9 us (28%)
  Pallas kernels  10.2 us (19%)
  waiting for transfers between devices  2.78 us (5%)
  between operations  0.93 us (2%)
  loops' own time  0.87 us (2%)
  local copies, waits for them, and re-layouts  0.68 us (1%)
    all_to_all x1, blocking collectives, on_device(): lax.all_to_all(parts[-1], 'space', split_axis=0, concat_axis=0, tiled=True)  23.4 us
    pallas_call x6, Pallas kernels, on_device(): pl.pallas_call(functools.partial(powers_kernel, stage, n, final), in_spec...  6.82 us
    ppermute x3, starting transfers between devices, on_device(): lax.ppermute(trace, 'probe', [(i, (i + k) % groups) for i in range(groups)])  5.67 us
    ppermute x1, starting transfers between devices, on_device(): below = lax.ppermute(up, 'space', [(i + 1, i) for i in range(strips - 1)])  5.11 us
    ppermute x2, starting transfers between devices, on_device(): lax.ppermute(dn, 'space', [(i, i + 1) for i in range(strips - 1)])  4.14 us
    ppermute x1, waiting for transfers between devices, on_device(): below = lax.ppermute(up, 'space', [(i + 1, i) for i in range(strips - 1)])  2.44 us
    pallas_call x1, Pallas kernels, on_device(): pl.pallas_call(prepare_kernel, in_specs=[HBM] * 4, out_specs=[VMEM] * (CH...  1.51 us
    pallas_call x1, Pallas kernels, on_device(): pl.pallas_call(combine_kernel, in_specs=[VMEM] * len(args), out_specs=HBM...  1.42 us
  transfers between devices with their start and end apart: 6, of which 2 were waited for; matrix products, arithmetic and copies ran while one was open for 0% of the time, Pallas kernels for 12%

profile of v4, /device:TPU:1, one launch (start us, length us, event | category | flops | bytes accessed | tf_op | source)
XLA Modules:
  0.0 53.8 jit_solution(12891919617526338824)
XLA Ops:
  0.6 1.5 %shard_map.59 = (f32[176,1024]{1,0:T(8,128)S(1)}, f32[48,1024]{1,0:T(8,128)S(1)}, f32[80,1024]{1,0:T(8,128)S(1)}, f32[96,1024]{1,0:T(8,128)S(1)}) custom-call(s32[48,8,1024]{2,1,0:T(8,128)} %signs_hbm.1, s32[8,1024]{1,0:T(8,128)} %mask_hbm.1, f32[8,1024]{1,0:T(8,128)} %weight_hbm.1, f32[8,1024]{1,0:T(8,128)} %mass_hbm.1), custom_call_target="tpu_custom_call" | custom-call | tf_op jit(solution)/shard_map/pallas_call | solution.py:372
  2.1 5.1 %collective-permute-start.4 = (f32[176,1024]{1,0:T(8,128)S(1)}, f32[176,1024]{1,0:T(8,128)S(1)}, u32[]{:S(2)}, u32[]{:S(2)}) collective-permute-start(f32[176,1024]{1,0:T(8,128)S(1)} %get-tuple-element.231.refs_0_), channel_id=1, source_target_pairs={{1,0},{2,1},{3,2},{4,3},{5,4},{6,5},{7,6},{8,7},{9,8},{10,9},{11,1... | collective-permute-start | bytes 2162696 | tf_op jit(solution)/shard_map/ppermute | solution.py:388
  7.3 1.9 %collective-permute-start.2 = (f32[96,1024]{1,0:T(8,128)S(1)}, f32[96,1024]{1,0:T(8,128)S(1)}, u32[]{:S(2)}, u32[]{:S(2)}) collective-permute-start(f32[96,1024]{1,0:T(8,128)S(1)} %get-tuple-element.233.refs_2_.refs_3_), channel_id=1, source_target_pairs={{0,1},{1,2},{2,3},{3,4},{4,5},{5,6},{6,7},{7,8},{8,9},{9,10},{10,1... | collective-permute-start | bytes 1179656 | tf_op jit(solution)/shard_map/ppermute | solution.py:391
  9.2 2.2 %collective-permute-start.3 = (f32[80,1024]{1,0:T(8,128)S(1)}, f32[80,1024]{1,0:T(8,128)S(1)}, u32[]{:S(2)}, u32[]{:S(2)}) collective-permute-start(f32[80,1024]{1,0:T(8,128)S(1)} %get-tuple-element.234.refs_2_), channel_id=1, source_target_pairs={{0,1},{1,2},{2,3},{3,4},{4,5},{5,6},{6,7},{7,8},{8,9},{9,10},{10,1... | collective-permute-start | bytes 983048 | tf_op jit(solution)/shard_map/ppermute | solution.py:391
  11.4 1.1 %shard_map.62 = (f32[6,24,1024]{2,1,0:T(8,128)S(1)}, f32[4,24,1024]{2,1,0:T(8,128)S(1)}, f32[2,24,1024]{2,1,0:T(8,128)S(1)}, f32[192,128]{1,0:T(8,128)S(1)}) custom-call(f32[176,1024]{1,0:T(8,128)S(1)} %get-tuple-element.231.refs_0_, f32[48,1024]{1,0:T(8,128)S(1)} %get-tuple-element.232.refs_1_, f32[80,1024]{1,0:T(8,128)S(1)} %get-tuple-element.234.refs_2_), custom_call_target="tpu_custom_call" | custom-call | tf_op jit(solution)/shard_map/pallas_call | solution.py:409
  12.5 1.1 %shard_map.60 = (f32[6,24,1024]{2,1,0:T(8,128)S(1)}, f32[4,24,1024]{2,1,0:T(8,128)S(1)}, f32[2,24,1024]{2,1,0:T(8,128)S(1)}, f32[192,128]{1,0:T(8,128)S(1)}) custom-call(f32[176,1024]{1,0:T(8,128)S(1)} %get-tuple-element.231.refs_0_, f32[48,1024]{1,0:T(8,128)S(1)} %get-tuple-element.232.refs_1_, f32[96,1024]{1,0:T(8,128)S(1)} %get-tuple-element.233.refs_2_.refs_3_), custom_call_target="tpu_custom_call" | custom-call | tf_op jit(solution)/shard_map/pallas_call | solution.py:409
  13.6 2.4 %collective-permute-done.4.refs_3_.refs_4_ = f32[176,1024]{1,0:T(8,128)S(1)} collective-permute-done((f32[176,1024]{1,0:T(8,128)S(1)}, f32[176,1024]{1,0:T(8,128)S(1)}, u32[]{:S(2)}, u32[]{:S(2)}) %collective-permute-start.4) | collective-permute-done | bytes 720928 | tf_op jit(solution)/shard_map/ppermute | solution.py:388
  16.0 1.0 %shard_map.63 = (f32[1,24,1024]{2,1,0:T(8,128)S(1)}, f32[2,24,1024]{2,1,0:T(8,128)S(1)}, f32[3,24,1024]{2,1,0:T(8,128)S(1)}, f32[192,128]{1,0:T(8,128)S(1)}) custom-call(f32[176,1024]{1,0:T(8,128)S(1)} %get-tuple-element.231.refs_0_, f32[48,1024]{1,0:T(8,128)S(1)} %get-tuple-element.232.refs_1_, f32[80,1024]{1,0:T(8,128)S(1)} %get-tuple-element.234.refs_2_, ...), custom_call_target="tpu_custom_call" | custom-call | tf_op jit(solution)/shard_map/pallas_call | solution.py:409
  17.1 0.3 collective-permute-done.3.refs_3_.refs_4_
  17.4 1.0 %shard_map.64 = (f32[1,24,1024]{2,1,0:T(8,128)S(1)}, f32[2,24,1024]{2,1,0:T(8,128)S(1)}, f32[3,24,1024]{2,1,0:T(8,128)S(1)}, f32[192,128]{1,0:T(8,128)S(1)}) custom-call(f32[176,1024]{1,0:T(8,128)S(1)} %get-tuple-element.231.refs_0_, f32[48,1024]{1,0:T(8,128)S(1)} %get-tuple-element.232.refs_1_, f32[80,1024]{1,0:T(8,128)S(1)} %get-tuple-element.234.refs_2_, ...), custom_call_target="tpu_custom_call" | custom-call | tf_op jit(solution)/shard_map/pallas_call | solution.py:409
  18.4 1.0 %shard_map.61 = (f32[1,24,1024]{2,1,0:T(8,128)S(1)}, f32[2,24,1024]{2,1,0:T(8,128)S(1)}, f32[3,24,1024]{2,1,0:T(8,128)S(1)}, f32[192,128]{1,0:T(8,128)S(1)}) custom-call(f32[176,1024]{1,0:T(8,128)S(1)} %get-tuple-element.231.refs_0_, f32[48,1024]{1,0:T(8,128)S(1)} %get-tuple-element.232.refs_1_, f32[96,1024]{1,0:T(8,128)S(1)} %get-tuple-element.233.refs_2_.refs_3_, ...), custom_call_target="tpu_custom_call" | custom-call | tf_op jit(solution)/shard_map/pallas_call | solution.py:409
  19.4 0.0 collective-permute-done.2.refs_3_
  19.4 1.6 %shard_map.65 = (f32[1,24,1024]{2,1,0:T(8,128)S(1)}, f32[2,24,1024]{2,1,0:T(8,128)S(1)}, f32[3,24,1024]{2,1,0:T(8,128)S(1)}, f32[64,1,384]{2,1,0:T(1,128)S(1)}) custom-call(f32[176,1024]{1,0:T(8,128)S(1)} %get-tuple-element.231.refs_0_, f32[48,1024]{1,0:T(8,128)S(1)} %get-tuple-element.232.refs_1_, f32[96,1024]{1,0:T(8,128)S(1)} %get-tuple-element.233.refs_2_.refs_3_, ...), custom_call_target="tpu_custom_call" | custom-call | tf_op jit(solution)/shard_map/pallas_call | solution.py:409
  21.1 23.4 %all_to_all.49.sums_ref = f32[64,1,384]{2,1,0:T(1,128)S(1)} all-to-all(f32[64,1,384]{2,1,0:T(1,128)S(1)} %get-tuple-element.246), channel_id=1, replica_groups=mesh['probe'=4,'space'=64] {'space'}, dimensions={0} | all-to-all | bytes 196608 | tf_op jit(solution)/shard_map/all_to_all | solution.py:419
  44.5 0.4 shard_map.66
  44.9 3.0 %collective-permute-start.5 = (f32[1,128]{1,0:T(1,128)S(1)}, f32[1,128]{1,0:T(1,128)S(1)}, u32[]{:S(2)}, u32[]{:S(2)}) collective-permute-start(f32[1,128]{1,0:T(1,128)S(1)} %get-tuple-element.247), channel_id=1, source_target_pairs={{0,128},{64,192},{128,0},{192,64},{1,129},{65,193},{129,1},{193,65... | collective-permute-start | bytes 1544 | tf_op jit(solution)/shard_map/ppermute | solution.py:431
  47.9 0.4 collective-permute-start.6
  48.3 2.3 %collective-permute-start.7 = (f32[1,128]{1,0:T(1,128)S(1)}, f32[1,128]{1,0:T(1,128)S(1)}, u32[]{:S(2)}, u32[]{:S(2)}) collective-permute-start(f32[1,128]{1,0:T(1,128)S(1)} %get-tuple-element.247), channel_id=1, source_target_pairs={{0,192},{64,0},{128,64},{192,128},{1,193},{65,1},{129,65},{193,129... | collective-permute-start | bytes 1544 | tf_op jit(solution)/shard_map/ppermute | solution.py:431
  50.6 0.0 copy-start.1
  50.6 0.0 copy-start.4
  50.6 0.0 copy-start.6
  50.6 0.0 copy-start.8
  50.6 1.4 %shard_map.67 = f32[48,8,1024]{2,1,0:T(8,128)} custom-call(f32[192,128]{1,0:T(8,128)S(1)} %get-tuple-element.248.coef_ref, f32[176,1024]{1,0:T(8,128)S(1)} %get-tuple-element.231.refs_0_, f32[48,1024]{1,0:T(8,128)S(1)} %get-tuple-element.232.refs_1_, f32[80,1024]{1,0:T(8,128)S(1)} %get-tuple-element.234.refs_2_, ...), custom_call_target="tpu_custom_call" | custom-call | flops 3145728 | bytes 7864320 | tf_op jit(solution)/shard_map/pallas_call | solution.py:438
  52.0 0.0 collective-permute-done.5
  52.1 0.0 collective-permute-done.6
  52.1 0.0 collective-permute-done.7
  52.1 0.7 %fusion.4 = (f32[1,1]{1,0:T(1,128)}, f32[1,1]{1,0:T(1,128)}, f32[1,1]{1,0:T(1,128)}) fusion(f32[1,128]{1,0:T(1,128)S(1)} %add_add_fusion), kind=kLoop, calls=%fused_computation.22 | loop fusion | bytes 24 | tf_op jit(solution)/shard_map/slice | solution.py:462
  52.8 0.0 copy-done.1
  52.8 0.0 copy-done.4
  52.8 0.0 copy-done.6
  52.8 0.0 copy-done.8
  52.8 0.9 %while.42 = (f32[]{:T(128)}, f32[]{:T(128)}, f32[48,8,1024]{2,1,0:T(8,128)}, f32[]{:T(128)}, s32[48,8,1024]{2,1,0:T(8,128)S(1)}, /*index=5*/s32[8,1024]{1,0:T(8,...) while((f32[]{:T(128)}, f32[]{:T(128)}, ...), condition=%wide.region_10.0_spmd, body=%wide.region_0.10_spmd.sunk | while | flops 17752440 | bytes 52235400 | solution.py:463
  (1 shorter events, 0.0 us)
Async XLA Ops:
  2.1 13.9 %collective-permute-start.4 = (f32[176,1024]{1,0:T(8,128)S(1)}, f32[176,1024]{1,0:T(8,128)S(1)}, u32[]{:S(2)}, u32[]{:S(2)}) collective-permute-start(f32[176,1024]{1,0:T(8,128)S(1)} %get-tuple-element.231.refs_0_), channel_id=1, source_target_pairs={{1,0},{2,1},{3,2},{4,3},{5,4},{6,5},{7,6},{8,7},{9,8},{10,9},{11,1... | collective-permute-start | bytes 2162696 | tf_op jit(solution)/shard_map/ppermute | solution.py:388
  7.3 12.2 %collective-permute-start.2 = (f32[96,1024]{1,0:T(8,128)S(1)}, f32[96,1024]{1,0:T(8,128)S(1)}, u32[]{:S(2)}, u32[]{:S(2)}) collective-permute-start(f32[96,1024]{1,0:T(8,128)S(1)} %get-tuple-element.233.refs_2_.refs_3_), channel_id=1, source_target_pairs={{0,1},{1,2},{2,3},{3,4},{4,5},{5,6},{6,7},{7,8},{8,9},{9,10},{10,1... | collective-permute-start | bytes 1179656 | tf_op jit(solution)/shard_map/ppermute | solution.py:391
  9.2 8.2 %collective-permute-start.3 = (f32[80,1024]{1,0:T(8,128)S(1)}, f32[80,1024]{1,0:T(8,128)S(1)}, u32[]{:S(2)}, u32[]{:S(2)}) collective-permute-start(f32[80,1024]{1,0:T(8,128)S(1)} %get-tuple-element.234.refs_2_), channel_id=1, source_target_pairs={{0,1},{1,2},{2,3},{3,4},{4,5},{5,6},{6,7},{7,8},{8,9},{9,10},{10,1... | collective-permute-start | bytes 983048 | tf_op jit(solution)/shard_map/ppermute | solution.py:391
  44.9 7.1 %collective-permute-start.5 = (f32[1,128]{1,0:T(1,128)S(1)}, f32[1,128]{1,0:T(1,128)S(1)}, u32[]{:S(2)}, u32[]{:S(2)}) collective-permute-start(f32[1,128]{1,0:T(1,128)S(1)} %get-tuple-element.247), channel_id=1, source_target_pairs={{0,128},{64,192},{128,0},{192,64},{1,129},{65,193},{129,1},{193,65... | collective-permute-start | bytes 1544 | tf_op jit(solution)/shard_map/ppermute | solution.py:431
  47.9 4.1 %collective-permute-start.6 = (f32[1,128]{1,0:T(1,128)S(1)}, f32[1,128]{1,0:T(1,128)S(1)}, u32[]{:S(2)}, u32[]{:S(2)}) collective-permute-start(f32[1,128]{1,0:T(1,128)S(1)} %get-tuple-element.247), channel_id=1, source_target_pairs={{0,64},{64,128},{128,192},{192,0},{1,65},{65,129},{129,193},{193,1... | collective-permute-start | bytes 1544 | tf_op jit(solution)/shard_map/ppermute | solution.py:431
  48.3 3.7 %collective-permute-start.7 = (f32[1,128]{1,0:T(1,128)S(1)}, f32[1,128]{1,0:T(1,128)S(1)}, u32[]{:S(2)}, u32[]{:S(2)}) collective-permute-start(f32[1,128]{1,0:T(1,128)S(1)} %get-tuple-element.247), channel_id=1, source_target_pairs={{0,192},{64,0},{128,64},{192,128},{1,193},{65,1},{129,65},{193,129... | collective-permute-start | bytes 1544 | tf_op jit(solution)/shard_map/ppermute | solution.py:431
  50.6 2.2 %copy-start.1 = (s32[48,8,1024]{2,1,0:T(8,128)S(1)}, s32[48,8,1024]{2,1,0:T(8,128)}, u32[]{:S(2)}) copy-start(s32[48,8,1024]{2,1,0:T(8,128)} %signs_hbm.1) | copy-start | bytes 4718596
  50.6 2.2 %copy-start.4 = (s32[8,1024]{1,0:T(8,128)S(1)}, s32[8,1024]{1,0:T(8,128)}, u32[]{:S(2)}) copy-start(s32[8,1024]{1,0:T(8,128)} %mask_hbm.1) | copy-start | bytes 98308
  50.6 2.2 %copy-start.6 = (f32[8,1024]{1,0:T(8,128)S(1)}, f32[8,1024]{1,0:T(8,128)}, u32[]{:S(2)}) copy-start(f32[8,1024]{1,0:T(8,128)} %weight_hbm.1) | copy-start | bytes 98308
  50.6 2.2 %copy-start.8 = (f32[8,1024]{1,0:T(8,128)S(1)}, f32[8,1024]{1,0:T(8,128)}, u32[]{:S(2)}) copy-start(f32[8,1024]{1,0:T(8,128)} %mass_hbm.1) | copy-start | bytes 98308

commit v5 on v4

--- a/solution.py
+++ b/solution.py
@@ -63,7 +63,7 @@
 
 
 def reach(n):
-    return (3, 4) if n % 2 == 0 else (4, 3)
+    return (4, 3) if n % 2 == 0 else (3, 4)
 
 
 def up_start(n, count):
@@ -176,7 +176,7 @@
         if level:
             if not 0 <= r < rows:
                 n = r - rows if r >= rows else r + above_rows - level
-                return halo[level], (n, slice(None))
+                return halo[level], (n, mine)
             by = owner(level, r, rows)
             source = own if by == stage else middle
             return source[level], (r - kept(by, level, rows)[0], mine)
@@ -197,9 +197,7 @@
             out.append(a + b)
         return out
 
-    def group(g, carry):
-        base = pl.multiple_of(g * GROUP, GROUP)
-
+    def group(base):
         def line(level, r):
             ref, index = where(level, r, base)
             return [ref[index + (at(c),)] for c in range(tiles)]
@@ -234,9 +232,9 @@
         for k, total in enumerate(totals):
             mine = pl.ds(k * probes + base, GROUP)
             part_ref[mine, :] = total + before_ref[mine, :] if stage else total
-        return carry
-
-    lax.fori_loop(0, probes // GROUP, group, 0)
+
+    for base in range(0, probes, GROUP):
+        group(base)
     part_ref[7 * probes :, :] = jnp.zeros((probes, LANES), jnp.float32)
     if not final:
         return
@@ -403,7 +401,8 @@
                 args.append(parts[0])
             outs = [shaped(kept(stage, level, rows)[1], count, columns) for level in range(1, ITERS)]
             outs.append(shaped(strips, 1, 8 * probes) if final else shaped(8 * count, LANES))
-            scratch = [pltpu.VMEM((size, GROUP, columns), jnp.float32) for size in (rows + 5, 3, 2, 1)]
+            scratch = [pltpu.VMEM((rows + 5, GROUP, columns), jnp.float32)]
+            scratch += [pltpu.VMEM((size, count, columns), jnp.float32) for size in (3, 2, 1)]
             if final:
                 scratch += [pltpu.VMEM((8 * probes, LANES), jnp.float32), pltpu.VMEM((8 * count, LANES), jnp.float32)]
             *fresh, parts[n] = pl.pallas_call(

time: 54.1 us -> 51.3 us (0.948)
  blocking collectives: 23.4 us -> 22 us
  Pallas kernels: 10.2 us -> 8.92 us
    all_to_all x1, blocking collectives: 23.4 us -> 22 us  [on_device(): lax.all_to_all(parts[-1], 'space', split_axis=0, concat_axis=0, tiled=True)]
    pallas_call x6, Pallas kernels: 6.82 us -> 5.56 us  [on_device(): pl.pallas_call(functools.partial(powers_kernel, stage, n, final), in_spec...]
  transfers between devices with their start and end apart: 6 -> 6, of which waited for: 2 -> 1; matrix products, arithmetic and copies ran while one was open for 0% -> 0% of each run, Pallas kernels for 12% -> 12%
where the time goes in v5:
time: 51.3 us; the launch traced here: 51.1 us
  blocking collectives  22 us (43%)
  starting transfers between devices  14.9 us (29%)
  Pallas kernels  8.92 us (17%)
  waiting for transfers between devices  2.76 us (5%)
  between operations  0.93 us (2%)
  loops' own time  0.87 us (2%)
  local copies, waits for them, and re-layouts  0.68 us (1%)
    all_to_all x1, blocking collectives, on_device(): lax.all_to_all(parts[-1], 'space', split_axis=0, concat_axis=0, tiled=True)  22 us
    ppermute x3, starting transfers between devices, on_device(): lax.ppermute(trace, 'probe', [(i, (i + k) % groups) for i in range(groups)])  5.67 us
    pallas_call x6, Pallas kernels, on_device(): pl.pallas_call(functools.partial(powers_kernel, stage, n, final), in_spec...  5.56 us
    ppermute x1, starting transfers between devices, on_device(): below = lax.ppermute(up, 'space', [(i + 1, i) for i in range(strips - 1)])  5.11 us
    ppermute x2, starting transfers between devices, on_device(): lax.ppermute(dn, 'space', [(i, i + 1) for i in range(strips - 1)])  4.14 us
    ppermute x1, waiting for transfers between devices, on_device(): below = lax.ppermute(up, 'space', [(i + 1, i) for i in range(strips - 1)])  2.75 us
    pallas_call x1, Pallas kernels, on_device(): pl.pallas_call(prepare_kernel, in_specs=[HBM] * 4, out_specs=[VMEM] * (CH...  1.51 us
    pallas_call x1, Pallas kernels, on_device(): pl.pallas_call(combine_kernel, in_specs=[VMEM] * len(args), out_specs=HBM...  1.42 us
  transfers between devices with their start and end apart: 6, of which 1 were waited for; matrix products, arithmetic and copies ran while one was open for 0% of the time, Pallas kernels for 12%

profile of v5, /device:TPU:1, one launch (start us, length us, event | category | flops | bytes accessed | tf_op | source)
XLA Modules:
  0.0 51.1 jit_solution(13677508093997160477)
XLA Ops:
  0.6 1.5 %shard_map.59 = (f32[176,1024]{1,0:T(8,128)S(1)}, f32[48,1024]{1,0:T(8,128)S(1)}, f32[104,1024]{1,0:T(8,128)S(1)}, f32[72,1024]{1,0:T(8,128)S(1)}) custom-call(s32[48,8,1024]{2,1,0:T(8,128)} %signs_hbm.1, s32[8,1024]{1,0:T(8,128)} %mask_hbm.1, f32[8,1024]{1,0:T(8,128)} %weight_hbm.1, f32[8,1024]{1,0:T(8,128)} %mass_hbm.1), custom_call_target="tpu_custom_call" | custom-call | tf_op jit(solution)/shard_map/pallas_call | solution.py:370
  2.1 5.1 %collective-permute-start.4 = (f32[176,1024]{1,0:T(8,128)S(1)}, f32[176,1024]{1,0:T(8,128)S(1)}, u32[]{:S(2)}, u32[]{:S(2)}) collective-permute-start(f32[176,1024]{1,0:T(8,128)S(1)} %get-tuple-element.231.refs_0_), channel_id=1, source_target_pairs={{1,0},{2,1},{3,2},{4,3},{5,4},{6,5},{7,6},{8,7},{9,8},{10,9},{11,1... | collective-permute-start | bytes 2162696 | tf_op jit(solution)/shard_map/ppermute | solution.py:386
  7.3 1.9 %collective-permute-start.3 = (f32[104,1024]{1,0:T(8,128)S(1)}, f32[104,1024]{1,0:T(8,128)S(1)}, u32[]{:S(2)}, u32[]{:S(2)}) collective-permute-start(f32[104,1024]{1,0:T(8,128)S(1)} %get-tuple-element.234.refs_2_), channel_id=1, source_target_pairs={{0,1},{1,2},{2,3},{3,4},{4,5},{5,6},{6,7},{7,8},{8,9},{9,10},{10,1... | collective-permute-start | bytes 1277960 | tf_op jit(solution)/shard_map/ppermute | solution.py:389
  9.2 2.2 %collective-permute-start.2 = (f32[72,1024]{1,0:T(8,128)S(1)}, f32[72,1024]{1,0:T(8,128)S(1)}, u32[]{:S(2)}, u32[]{:S(2)}) collective-permute-start(f32[72,1024]{1,0:T(8,128)S(1)} %get-tuple-element.233.refs_2_.refs_3_), channel_id=1, source_target_pairs={{0,1},{1,2},{2,3},{3,4},{4,5},{5,6},{6,7},{7,8},{8,9},{9,10},{10,1... | collective-permute-start | bytes 884744 | tf_op jit(solution)/shard_map/ppermute | solution.py:389
  11.4 0.9 %shard_map.62 = (f32[6,24,1024]{2,1,0:T(8,128)S(1)}, f32[4,24,1024]{2,1,0:T(8,128)S(1)}, f32[2,24,1024]{2,1,0:T(8,128)S(1)}, f32[192,128]{1,0:T(8,128)S(1)}) custom-call(f32[176,1024]{1,0:T(8,128)S(1)} %get-tuple-element.231.refs_0_, f32[48,1024]{1,0:T(8,128)S(1)} %get-tuple-element.232.refs_1_, f32[104,1024]{1,0:T(8,128)S(1)} %get-tuple-element.234.refs_2_), custom_call_target="tpu_custom_call" | custom-call | tf_op jit(solution)/shard_map/pallas_call | solution.py:408
  12.4 0.9 %shard_map.60 = (f32[6,24,1024]{2,1,0:T(8,128)S(1)}, f32[4,24,1024]{2,1,0:T(8,128)S(1)}, f32[2,24,1024]{2,1,0:T(8,128)S(1)}, f32[192,128]{1,0:T(8,128)S(1)}) custom-call(f32[176,1024]{1,0:T(8,128)S(1)} %get-tuple-element.231.refs_0_, f32[48,1024]{1,0:T(8,128)S(1)} %get-tuple-element.232.refs_1_, f32[72,1024]{1,0:T(8,128)S(1)} %get-tuple-element.233.refs_2_.refs_3_), custom_call_target="tpu_custom_call" | custom-call | tf_op jit(solution)/shard_map/pallas_call | solution.py:408
  13.3 2.7 %collective-permute-done.4.refs_3_.refs_4_ = f32[176,1024]{1,0:T(8,128)S(1)} collective-permute-done((f32[176,1024]{1,0:T(8,128)S(1)}, f32[176,1024]{1,0:T(8,128)S(1)}, u32[]{:S(2)}, u32[]{:S(2)}) %collective-permute-start.4) | collective-permute-done | bytes 720928 | tf_op jit(solution)/shard_map/ppermute | solution.py:386
  16.0 0.8 %shard_map.63 = (f32[1,24,1024]{2,1,0:T(8,128)S(1)}, f32[2,24,1024]{2,1,0:T(8,128)S(1)}, f32[3,24,1024]{2,1,0:T(8,128)S(1)}, f32[192,128]{1,0:T(8,128)S(1)}) custom-call(f32[176,1024]{1,0:T(8,128)S(1)} %get-tuple-element.231.refs_0_, f32[48,1024]{1,0:T(8,128)S(1)} %get-tuple-element.232.refs_1_, f32[104,1024]{1,0:T(8,128)S(1)} %get-tuple-element.234.refs_2_, ...), custom_call_target="tpu_custom_call" | custom-call | tf_op jit(solution)/shard_map/pallas_call | solution.py:408
  16.8 0.0 collective-permute-done.3.refs_3_.refs_4_
  16.9 1.1 %shard_map.64 = (f32[1,24,1024]{2,1,0:T(8,128)S(1)}, f32[2,24,1024]{2,1,0:T(8,128)S(1)}, f32[3,24,1024]{2,1,0:T(8,128)S(1)}, f32[192,128]{1,0:T(8,128)S(1)}) custom-call(f32[176,1024]{1,0:T(8,128)S(1)} %get-tuple-element.231.refs_0_, f32[48,1024]{1,0:T(8,128)S(1)} %get-tuple-element.232.refs_1_, f32[104,1024]{1,0:T(8,128)S(1)} %get-tuple-element.234.refs_2_, ...), custom_call_target="tpu_custom_call" | custom-call | tf_op jit(solution)/shard_map/pallas_call | solution.py:408
  18.0 0.9 %shard_map.61 = (f32[1,24,1024]{2,1,0:T(8,128)S(1)}, f32[2,24,1024]{2,1,0:T(8,128)S(1)}, f32[3,24,1024]{2,1,0:T(8,128)S(1)}, f32[192,128]{1,0:T(8,128)S(1)}) custom-call(f32[176,1024]{1,0:T(8,128)S(1)} %get-tuple-element.231.refs_0_, f32[48,1024]{1,0:T(8,128)S(1)} %get-tuple-element.232.refs_1_, f32[72,1024]{1,0:T(8,128)S(1)} %get-tuple-element.233.refs_2_.refs_3_, ...), custom_call_target="tpu_custom_call" | custom-call | tf_op jit(solution)/shard_map/pallas_call | solution.py:408
  18.8 0.0 collective-permute-done.2.refs_3_
  18.8 0.9 %shard_map.65 = (f32[1,24,1024]{2,1,0:T(8,128)S(1)}, f32[2,24,1024]{2,1,0:T(8,128)S(1)}, f32[3,24,1024]{2,1,0:T(8,128)S(1)}, f32[64,1,384]{2,1,0:T(1,128)S(1)}) custom-call(f32[176,1024]{1,0:T(8,128)S(1)} %get-tuple-element.231.refs_0_, f32[48,1024]{1,0:T(8,128)S(1)} %get-tuple-element.232.refs_1_, f32[72,1024]{1,0:T(8,128)S(1)} %get-tuple-element.233.refs_2_.refs_3_, ...), custom_call_target="tpu_custom_call" | custom-call | tf_op jit(solution)/shard_map/pallas_call | solution.py:408
  19.8 22.0 %all_to_all.49.sums_ref = f32[64,1,384]{2,1,0:T(1,128)S(1)} all-to-all(f32[64,1,384]{2,1,0:T(1,128)S(1)} %get-tuple-element.246), channel_id=1, replica_groups=mesh['probe'=4,'space'=64] {'space'}, dimensions={0} | all-to-all | bytes 196608 | tf_op jit(solution)/shard_map/all_to_all | solution.py:418
  41.8 0.4 shard_map.66
  42.2 3.0 %collective-permute-start.5 = (f32[1,128]{1,0:T(1,128)S(1)}, f32[1,128]{1,0:T(1,128)S(1)}, u32[]{:S(2)}, u32[]{:S(2)}) collective-permute-start(f32[1,128]{1,0:T(1,128)S(1)} %get-tuple-element.247), channel_id=1, source_target_pairs={{0,128},{64,192},{128,0},{192,64},{1,129},{65,193},{129,1},{193,65... | collective-permute-start | bytes 1544 | tf_op jit(solution)/shard_map/ppermute | solution.py:430
  45.2 0.4 collective-permute-start.6
  45.6 2.3 %collective-permute-start.7 = (f32[1,128]{1,0:T(1,128)S(1)}, f32[1,128]{1,0:T(1,128)S(1)}, u32[]{:S(2)}, u32[]{:S(2)}) collective-permute-start(f32[1,128]{1,0:T(1,128)S(1)} %get-tuple-element.247), channel_id=1, source_target_pairs={{0,192},{64,0},{128,64},{192,128},{1,193},{65,1},{129,65},{193,129... | collective-permute-start | bytes 1544 | tf_op jit(solution)/shard_map/ppermute | solution.py:430
  47.9 0.0 copy-start.1
  47.9 0.0 copy-start.4
  47.9 0.0 copy-start.6
  47.9 0.0 copy-start.8
  47.9 1.4 %shard_map.67 = f32[48,8,1024]{2,1,0:T(8,128)} custom-call(f32[192,128]{1,0:T(8,128)S(1)} %get-tuple-element.248.coef_ref, f32[176,1024]{1,0:T(8,128)S(1)} %get-tuple-element.231.refs_0_, f32[48,1024]{1,0:T(8,128)S(1)} %get-tuple-element.232.refs_1_, f32[104,1024]{1,0:T(8,128)S(1)} %get-tuple-element.234.refs_2_, ...), custom_call_target="tpu_custom_call" | custom-call | flops 3145728 | bytes 7864320 | tf_op jit(solution)/shard_map/pallas_call | solution.py:437
  49.3 0.0 collective-permute-done.5
  49.3 0.0 collective-permute-done.6
  49.3 0.0 collective-permute-done.7
  49.4 0.7 %fusion.4 = (f32[1,1]{1,0:T(1,128)}, f32[1,1]{1,0:T(1,128)}, f32[1,1]{1,0:T(1,128)}) fusion(f32[1,128]{1,0:T(1,128)S(1)} %add_add_fusion), kind=kLoop, calls=%fused_computation.22 | loop fusion | bytes 24 | tf_op jit(solution)/shard_map/slice | solution.py:461
  50.0 0.0 copy-done.1
  50.0 0.0 copy-done.4
  50.0 0.0 copy-done.6
  50.0 0.0 copy-done.8
  50.1 0.9 %while.42 = (f32[]{:T(128)}, f32[]{:T(128)}, f32[48,8,1024]{2,1,0:T(8,128)}, f32[]{:T(128)}, s32[48,8,1024]{2,1,0:T(8,128)S(1)}, /*index=5*/s32[8,1024]{1,0:T(8,...) while((f32[]{:T(128)}, f32[]{:T(128)}, ...), condition=%wide.region_10.0_spmd, body=%wide.region_0.10_spmd.sunk | while | flops 17752440 | bytes 52235400 | solution.py:462
  (1 shorter events, 0.0 us)
Async XLA Ops:
  2.1 13.9 %collective-permute-start.4 = (f32[176,1024]{1,0:T(8,128)S(1)}, f32[176,1024]{1,0:T(8,128)S(1)}, u32[]{:S(2)}, u32[]{:S(2)}) collective-permute-start(f32[176,1024]{1,0:T(8,128)S(1)} %get-tuple-element.231.refs_0_), channel_id=1, source_target_pairs={{1,0},{2,1},{3,2},{4,3},{5,4},{6,5},{7,6},{8,7},{9,8},{10,9},{11,1... | collective-permute-start | bytes 2162696 | tf_op jit(solution)/shard_map/ppermute | solution.py:386
  7.3 9.6 %collective-permute-start.3 = (f32[104,1024]{1,0:T(8,128)S(1)}, f32[104,1024]{1,0:T(8,128)S(1)}, u32[]{:S(2)}, u32[]{:S(2)}) collective-permute-start(f32[104,1024]{1,0:T(8,128)S(1)} %get-tuple-element.234.refs_2_), channel_id=1, source_target_pairs={{0,1},{1,2},{2,3},{3,4},{4,5},{5,6},{6,7},{7,8},{8,9},{9,10},{10,1... | collective-permute-start | bytes 1277960 | tf_op jit(solution)/shard_map/ppermute | solution.py:389
  9.2 9.6 %collective-permute-start.2 = (f32[72,1024]{1,0:T(8,128)S(1)}, f32[72,1024]{1,0:T(8,128)S(1)}, u32[]{:S(2)}, u32[]{:S(2)}) collective-permute-start(f32[72,1024]{1,0:T(8,128)S(1)} %get-tuple-element.233.refs_2_.refs_3_), channel_id=1, source_target_pairs={{0,1},{1,2},{2,3},{3,4},{4,5},{5,6},{6,7},{7,8},{8,9},{9,10},{10,1... | collective-permute-start | bytes 884744 | tf_op jit(solution)/shard_map/ppermute | solution.py:389
  42.2 7.1 %collective-permute-start.5 = (f32[1,128]{1,0:T(1,128)S(1)}, f32[1,128]{1,0:T(1,128)S(1)}, u32[]{:S(2)}, u32[]{:S(2)}) collective-permute-start(f32[1,128]{1,0:T(1,128)S(1)} %get-tuple-element.247), channel_id=1, source_target_pairs={{0,128},{64,192},{128,0},{192,64},{1,129},{65,193},{129,1},{193,65... | collective-permute-start | bytes 1544 | tf_op jit(solution)/shard_map/ppermute | solution.py:430
  45.2 4.1 %collective-permute-start.6 = (f32[1,128]{1,0:T(1,128)S(1)}, f32[1,128]{1,0:T(1,128)S(1)}, u32[]{:S(2)}, u32[]{:S(2)}) collective-permute-start(f32[1,128]{1,0:T(1,128)S(1)} %get-tuple-element.247), channel_id=1, source_target_pairs={{0,64},{64,128},{128,192},{192,0},{1,65},{65,129},{129,193},{193,1... | collective-permute-start | bytes 1544 | tf_op jit(solution)/shard_map/ppermute | solution.py:430
  45.6 3.7 %collective-permute-start.7 = (f32[1,128]{1,0:T(1,128)S(1)}, f32[1,128]{1,0:T(1,128)S(1)}, u32[]{:S(2)}, u32[]{:S(2)}) collective-permute-start(f32[1,128]{1,0:T(1,128)S(1)} %get-tuple-element.247), channel_id=1, source_target_pairs={{0,192},{64,0},{128,64},{192,128},{1,193},{65,1},{129,65},{193,129... | collective-permute-start | bytes 1544 | tf_op jit(solution)/shard_map/ppermute | solution.py:430
  47.9 2.2 %copy-start.1 = (s32[48,8,1024]{2,1,0:T(8,128)S(1)}, s32[48,8,1024]{2,1,0:T(8,128)}, u32[]{:S(2)}) copy-start(s32[48,8,1024]{2,1,0:T(8,128)} %signs_hbm.1) | copy-start | bytes 4718596
  47.9 2.2 %copy-start.4 = (s32[8,1024]{1,0:T(8,128)S(1)}, s32[8,1024]{1,0:T(8,128)}, u32[]{:S(2)}) copy-start(s32[8,1024]{1,0:T(8,128)} %mask_hbm.1) | copy-start | bytes 98308
  47.9 2.2 %copy-start.6 = (f32[8,1024]{1,0:T(8,128)S(1)}, f32[8,1024]{1,0:T(8,128)}, u32[]{:S(2)}) copy-start(f32[8,1024]{1,0:T(8,128)} %weight_hbm.1) | copy-start | bytes 98308
  47.9 2.2 %copy-start.8 = (f32[8,1024]{1,0:T(8,128)S(1)}, f32[8,1024]{1,0:T(8,128)}, u32[]{:S(2)}) copy-start(f32[8,1024]{1,0:T(8,128)} %mass_hbm.1) | copy-start | bytes 98308
